TPU v7x, 128 devices: a whole 4x4x4 slice. The times are simulated.
128 devices in a mesh: obs: 4 (over y), cell: 32 (over z, x, core).
Axes of the slice: x: 4, y: 4, z: 4, core: 2. Of those that a mesh axis runs over, the one named last changes fastest.
Arguments:
- log_k: bfloat16 [6291456, 128], P(('obs', 'cell')), may hold values from -6 to 6
- heads_pred: bfloat16 [65536, 128], P(('obs', 'cell')), may hold values from -6 to 6
- slot_well: int32 [65536], P(('obs', 'cell')), may hold values from 0 to 16383, as said below
- tile_count: int32 [128], P(('obs', 'cell')), may hold values from 16 to 512, as said below
- obs_values: float32 [16384, 128], P(('obs', 'cell')), may hold values from -9 to 9
- obs_std: float32 [16384], P(('obs', 'cell')), may hold values from 0.5 to 2
- loc_blocks: int32 [32, 8], replicated, may hold values from 0 to 127, all different within a row
- taper: float32 [32, 8], replicated, may hold values from 0.3 to 1
- lambdas: float32 [4], replicated, may hold values from 0.1 to 10
Outputs:
- posterior: bfloat16 [6291456, 128], P(('obs', 'cell'))
- change_norms: float32 [128, 4, 128], P(('obs', 'cell'))
Inputs may be any that keep to these rules, and one draw needn't show every extreme that they name: `slot_well`: slots below a cell block's count hold the wells lying in that block in increasing order; every well lies in exactly one cell block; other slots hold 0. No cell block holds more than 16 wells of one observation block, and some pairs hold exactly 16. `tile_count`: some cell blocks hold exactly 512 wells. `loc_blocks`: each row names 8 different blocks, and every block is named by some tile.
All inputs are finite; a program needn't handle non-finite values.
Results may differ from a plain program's by a relative error of at most 0.0095.
Values may be sent and summed in bfloat16 or wider, within the bound.
No kernel may reach another device: no remote copies, remote signals or barrier semaphores. Data moves between devices by JAX's collectives and lax.ppermute only.
A program may use at most 256 MiB of HBM per device.

v0:
```python
import jax
import jax.numpy as jnp
from jax import lax
from jax.sharding import PartitionSpec as P

CAP = 16


def cut_along(array, dim, devices):
    before, after = (array.shape[:dim], array.shape[dim + 1 :])
    return jnp.moveaxis(array.reshape(*before, devices, -1, *after), dim, 0)


def laid_out(blocks, dim):
    blocks = jnp.moveaxis(blocks, 0, dim)
    lengths = blocks.shape
    return blocks.reshape(*lengths[:dim], lengths[dim] * lengths[dim + 1], *lengths[dim + 2 :])


def exchange_both(array, axis, axes, splits, concats):
    sizes = [lax.axis_size(a) for a in axes]
    blocks = cut_along(array, splits[0], sizes[0])
    blocks = jnp.moveaxis(cut_along(blocks, splits[1] + 1, sizes[1]), 0, 1)
    inside = blocks.shape[2:]
    blocks = blocks.reshape(-1, *inside)
    blocks = lax.all_to_all(blocks, axis, split_axis=0, concat_axis=0, tiled=True)
    blocks = laid_out(blocks.reshape(*sizes, *inside), concats[0] + 1)
    return laid_out(blocks, concats[1])


def summed_on_arrival(array, axis, dim):
    devices = lax.axis_size(axis)
    blocks = lax.all_to_all(cut_along(array, dim, devices), axis, 0, 0, tiled=True)
    return jnp.sum(blocks, axis=0)


def sent_to_all(array, axis):
    copies = jnp.broadcast_to(array, (lax.axis_size(axis), *array.shape))
    return lax.all_to_all(copies, axis, split_axis=0, concat_axis=0, tiled=True)


def gather_directly(array, axis, dim):
    blocks = sent_to_all(array, axis)
    return laid_out(blocks, dim)


def solve_lambdas(curvature, right_side, lambda_values):
    member_count = curvature.shape[0]
    identity = jnp.eye(member_count, dtype=jnp.float32)
    shifts = (1.0 + lambda_values) * (member_count - 1)
    systems = curvature[None] + shifts[:, None, None] * identity[None]
    factor = jnp.linalg.cholesky(systems)
    targets = right_side[None]
    return jax.scipy.linalg.cho_solve((factor, True), targets).astype(jnp.bfloat16)


def on_device(
    log_k, heads_pred, slot_well, tile_count, obs_values, obs_std, loc_blocks, taper, lambdas
):
    n_obs = lax.axis_size("obs")
    n_cell = lax.axis_size("cell")
    device_total = n_obs * n_cell
    slot_total = slot_well.shape[0]
    member_count = heads_pred.shape[1]
    wells_dev = obs_values.shape[0]
    capacity = CAP
    positions = jnp.arange(slot_total, dtype=jnp.int32)
    is_valid = positions < tile_count[0]
    owner_block = slot_well // wells_dev
    owner_row = slot_well % wells_dev
    earlier = jnp.sum(
        (is_valid[None, :] & (owner_block[None, :] < owner_block[:, None])).astype(jnp.int32),
        axis=1,
    )
    slot_rank = positions - earlier
    send_index = jnp.where(is_valid, owner_block * capacity + slot_rank, device_total * capacity)
    send_heads = (
        jnp.zeros((device_total * capacity, member_count), jnp.bfloat16)
        .at[send_index]
        .set(heads_pred, mode="drop")
    )
    send_place = (
        jnp.full((device_total * capacity,), wells_dev, jnp.int32)
        .at[send_index]
        .set(owner_row, mode="drop")
    )
    recv_heads, recv_place = (
        exchange_both(
            send_heads.reshape(n_obs, n_cell, capacity, member_count),
            ("obs", "cell"),
            ("obs", "cell"),
            (0, 1),
            (0, 1),
        ),
        exchange_both(
            send_place.reshape(n_obs, n_cell, capacity),
            ("obs", "cell"),
            ("obs", "cell"),
            (0, 1),
            (0, 1),
        ),
    )
    predicted = (
        jnp.zeros((wells_dev, member_count), jnp.float32)
        .at[recv_place.reshape(-1)]
        .set(recv_heads.reshape(-1, member_count).astype(jnp.float32), mode="drop")
    )
    member_mean = jnp.mean(predicted, axis=1, keepdims=True)
    scaled = (predicted - member_mean) / obs_std[:, None]
    innovation = (obs_values - predicted) / obs_std[:, None]
    joined = jnp.concatenate([scaled, innovation], axis=1)
    block_gram = jnp.dot(
        scaled.T, joined, precision=lax.Precision.HIGHEST, preferred_element_type=jnp.float32
    )
    cell_place = lax.axis_index("cell")
    tile_range = jnp.arange(n_cell, dtype=jnp.int32)
    band_rows = member_count // n_obs
    banded = lax.all_to_all(
        block_gram.reshape(n_obs, band_rows, 2 * member_count),
        "obs",
        split_axis=0,
        concat_axis=0,
        tiled=True,
    )
    column_blocks = jnp.arange(n_obs, dtype=jnp.int32) * n_cell + cell_place
    column_weight = jnp.sum(
        taper[:, :, None]
        * (loc_blocks[:, :, None] == column_blocks[None, None, :]).astype(jnp.float32),
        axis=1,
    )
    dest_index = jnp.arange(band_rows * lax.axis_size("cell") // band_rows, dtype=jnp.int32)
    selector = (dest_index[:, None] == tile_range[None, :]).astype(jnp.float32)
    weight_rows = jnp.sum(selector[:, :, None] * column_weight[None, :, :], axis=1)
    terms = jnp.sum(weight_rows[:, :, None, None] * banded[None], axis=1)
    band_part = summed_on_arrival(
        terms.reshape(band_rows * lax.axis_size("cell"), 2 * member_count), "cell", 0
    )
    tile_gram = gather_directly(band_part, "obs", 0)
    curvature = tile_gram[:, :member_count]
    right_side = tile_gram[:, member_count:]
    lambda_total = lambdas.shape[0]
    share = lambda_total // n_obs
    own_values = lax.dynamic_slice_in_dim(lambdas, lax.axis_index("obs") * share, share, 0)
    own_transforms = solve_lambdas(curvature, right_side, own_values)
    transforms = gather_directly(own_transforms, "obs", 0)
    field = log_k.astype(jnp.float32)
    anomalies = (field - jnp.mean(field, axis=1, keepdims=True)).astype(jnp.bfloat16)
    joined_transforms = jnp.transpose(transforms, (1, 0, 2)).reshape(
        member_count, lambda_total * member_count
    )
    change = jnp.dot(anomalies, joined_transforms, preferred_element_type=jnp.float32)
    change = change.reshape(field.shape[0], lambda_total, member_count)
    updated = (field + change[:, 0, :]).astype(jnp.bfloat16)
    change_norms = jnp.sum(change * change, axis=0)
    return (updated, change_norms[None])


def solution(mesh):
    return jax.shard_map(
        on_device,
        mesh=mesh,
        in_specs=(
            P(("obs", "cell"), None),
            P(("obs", "cell"), None),
            P(("obs", "cell")),
            P(("obs", "cell")),
            P(("obs", "cell"), None),
            P(("obs", "cell")),
            P(),
            P(),
            P(),
        ),
        out_specs=(P(("obs", "cell"), None), P(("obs", "cell"), None, None)),
        check_vma=False,
    )
```

profile of v0, /device:TPU:0, one launch (start us, length us, event | category | flops | bytes accessed | tf_op | source)
XLA Modules:
  0.0 188.8 jit_solution(5651062833701499530)
XLA Ops:
  0.6 0.0 copy-start
  1.3 0.7 add_select_fusion
  2.0 0.3 convert_reduce_fusion.1
  2.3 2.5 %scatter_custom_fusion = s32[2048]{0:T(1024)S(1)} fusion(s32[512]{0:T(512)S(1)} %compare_select_fusion.1, s32[512]{0:T(512)S(1)} %get-tuple-element.4, s32[]{:T(128)} %constant.100.clone.1), kind=kCustom, calls=%fused_computation.48 | custom fusion | bytes 8196 | tf_op jit(solution)/shard_map/scatter | solution.py:85
  4.8 0.7 reshape_transpose_transpose_reshape_reshape_reshape.6
  5.5 11.2 %all-to-all-start = ((s32[128,1,1,16]{3,2,1,0:T(1,128)}), s32[128,1,1,16]{3,2,1,0:T(1,128)S(1)}, u32[]{:S(2)}, u32[]{:S(2)}) async-start(s32[128,1,1,16]{3,2,1,0:T(1,128)} %bitcast.2), calls=%async_computation | async-start | bytes 131072 | tf_op jit(solution)/shard_map/all_to_all | solution.py:26
  16.7 0.8 select_reduce_fusion.1
  17.5 2.9 %scatter_custom_fusion.1 = bf16[2048,128]{1,0:T(8,128)(2,1)} fusion(s32[512]{0:T(512)S(1)} %compare_select_fusion.1, bf16[512,128]{1,0:T(8,128)(2,1)} %param.10, bf16[]{:T(256)} %constant.108.clone.1), kind=kCustom, calls=%fused_computation.18 | custom fusion | bytes 524800 | tf_op jit(solution)/shard_map/scatter | solution.py:80
  20.4 5.6 %all-to-all-done = s32[128,1,1,16]{3,2,1,0:T(1,128)S(1)} async-done(((s32[128,1,1,16]{3,2,1,0:T(1,128)}), s32[128,1,1,16]{3,2,1,0:T(1,128)S(1)}, u32[]{:S(2)}, u32[]{:S(2)}) %all-to-all-start) | async-done | bytes 8224 | tf_op jit(solution)/shard_map/all_to_all | solution.py:26
  26.0 4.8 %all-to-all-start.1 = ((bf16[128,1,1,16,128]{4,3,2,1,0:T(8,128)(2,1)}), bf16[128,1,1,16,128]{4,3,2,1,0:T(8,128)(2,1)S(1)}, u32[]{:S(2)}, u32[]{:S(2)}) async-start(bf16[128,1,1,16,128]{4,3,2,1,0:T(8,128)(2,1)} %bitcast.9), calls=%async_computation.1 | async-start | bytes 1048576 | tf_op jit(solution)/shard_map/all_to_all | solution.py:26
  30.8 0.1 reshape_reshape.4
  30.9 13.4 %all-to-all-done.1 = bf16[128,1,1,16,128]{4,3,2,1,0:T(8,128)(2,1)S(1)} async-done(((bf16[128,1,1,16,128]{4,3,2,1,0:T(8,128)(2,1)}), bf16[128,1,1,16,128]{4,3,2,1,0:T(8,128)(2,1)S(1)}, u32[]{:S(2)}, u32[]{:S(2)}) %all-to-all-start.1) | async-done | bytes 524320 | tf_op jit(solution)/shard_map/all_to_all | solution.py:26
  44.3 5.6 %scatter_custom_fusion.2 = f32[128,128]{1,0:T(8,128)S(1)} fusion(s32[2048]{0:T(1024)S(1)} %bitcast.78, bf16[2048,128]{1,0:T(8,128)(2,1)S(1)} %bitcast.74, f32[]{:T(128)} %constant.96.clone.1), kind=kCustom, calls=%fused_computation.15 | custom fusion | flops 262144 | bytes 589828 | tf_op jit(solution)/shard_map/scatter | solution.py:106
  49.9 0.1 reduce_sum.76
  50.1 0.9 subtract_divide_fusion
  51.0 1.0 fusion.10
  52.0 3.3 %all-to-all-start.2 = ((f32[4,32,256]{2,1,0:T(8,128)}), f32[4,32,256]{2,1,0:T(8,128)S(1)}, u32[]{:S(2)}, u32[]{:S(2)}) async-start(f32[4,32,256]{2,1,0:T(8,128)} %bitcast.15), calls=%async_computation.2 | async-start | bytes 262144 | tf_op jit(solution)/shard_map/all_to_all | solution.py:118
  55.3 0.1 multiply_reduce_fusion.2
  55.4 0.1 copy.30
  55.5 5.8 %all-to-all-done.2 = f32[4,32,256]{2,1,0:T(8,128)S(1)} async-done(((f32[4,32,256]{2,1,0:T(8,128)}), f32[4,32,256]{2,1,0:T(8,128)S(1)}, u32[]{:S(2)}, u32[]{:S(2)}) %all-to-all-start.2) | async-done | bytes 131104 | tf_op jit(solution)/shard_map/all_to_all | solution.py:118
  61.2 0.6 multiply_reduce_fusion.1
  61.8 20.9 %all_to_all.30 = f32[32,32,256]{2,1,0:T(8,128)S(1)} all-to-all(f32[32,32,256]{2,1,0:T(8,128)S(1)} %multiply_reduce_fusion.1), channel_id=1, replica_groups=mesh['obs'=4,'cell'=32] {'cell'}, dimensions={0} | all-to-all | bytes 2097152 | tf_op jit(solution)/shard_map/all_to_all | solution.py:33
  82.7 0.1 reduce_sum.78
  82.7 0.7 broadcast_in_dim.23
  83.4 3.5 %all-to-all-start.4 = ((f32[4,32,256]{2,1,0:T(8,128)}), f32[4,32,256]{2,1,0:T(8,128)S(1)}, u32[]{:S(2)}, u32[]{:S(2)}) async-start(f32[4,32,256]{2,1,0:T(8,128)} %broadcast_in_dim.23), calls=%async_computation.4 | async-start | bytes 262144 | tf_op jit(solution)/shard_map/all_to_all | solution.py:39
  86.9 7.6 %convert_reduce_fusion = f32[49152]{0:T(1024)S(1)} fusion(bf16[49152,128]{1,0:T(8,128)(2,1)} %param.9), kind=kLoop, calls=%fused_computation.6 | loop fusion | flops 12533760 | bytes 12779520 | tf_op jit(solution)/shard_map/reduce_sum | solution.py:147
  94.5 0.0 copy-done
  94.5 0.6 dynamic_slice.3
  95.8 0.0 all-to-all-done.4
  95.8 0.1 copy.37
  95.9 0.1 copy.35
  96.1 11.7 %custom-call.11 = f32[1,128,128]{2,1,0:T(8,128)S(1)} custom-call(f32[1,128,128]{2,1,0:T(8,128)S(1)} %fusion.17), custom_call_target="Cholesky" | custom-call | tf_op jit(solution)/shard_map/jit(cholesky)/cholesky | solution.py:52
  107.8 0.6 compare_reduce_fusion
  108.4 0.7 select_select_fusion
  109.1 9.8 %custom-call.12 = f32[1,128,128]{1,2,0:T(8,128)S(1)} custom-call(f32[1,128,128]{2,1,0:T(8,128)S(1)} %select_select_fusion), custom_call_target="InvertDiagBlocksLowerTriangular" | custom-call | tf_op jit(solution)/shard_map/jit(_cho_solve)/triangular_solve | solution.py:54
  118.9 0.3 fusion.15
  119.2 0.2 convolution_convert_fusion
  119.4 0.1 copy.36
  119.5 0.7 broadcast_in_dim.24
  120.2 4.6 %all-to-all-start.5 = ((bf16[4,1,128,128]{2,3,1,0:T(8,128)(2,1)}), bf16[4,1,128,128]{2,3,1,0:T(8,128)(2,1)S(1)}, u32[]{:S(2)}, u32[]{:S(2)}) async-start(bf16[4,1,128,128]{2,3,1,0:T(8,128)(2,1)} %broadcast_in_dim.24), calls=%async_computation.5 | async-start | bytes 262144 | tf_op jit(solution)/shard_map/all_to_all | solution.py:39
  124.8 6.0 %all-to-all-done.5 = bf16[4,1,128,128]{2,3,1,0:T(8,128)(2,1)S(1)} async-done(((bf16[4,1,128,128]{2,3,1,0:T(8,128)(2,1)}), bf16[4,1,128,128]{2,3,1,0:T(8,128)(2,1)S(1)}, u32[]{:S(2)}, u32[]{:S(2)}) %all-to-all-start.5) | async-done | bytes 131104 | tf_op jit(solution)/shard_map/all_to_all | solution.py:39
  130.8 40.6 %multiply_reduce_fusion = (f32[4,128]{1,0:T(4,128)}, f32[49152,4,128]{2,0,1:T(8,128)}) fusion(bf16[4,1,128,128]{2,3,1,0:T(8,128)(2,1)S(1)} %all-to-all-done.5, bf16[49152,128]{1,0:T(8,128)(2,1)} %param.9, f32[49152]{0:T(1024)S(1)} %broadcast_multiply_fusion), kind=kOutput, calls=%fused_computation.3 | convolution fusion | flops 6511656448 | bytes 113575936 | tf_op jit(solution)/shard_map/dot_general | solution.py:151
  171.4 17.4 %fusion.1 = bf16[49152,128]{1,0:T(8,128)(2,1)} fusion(bf16[49152,128]{1,0:T(8,128)(2,1)} %param.9, f32[49152,4,128]{2,0,1:T(8,128)} %get-tuple-element.7), kind=kLoop, calls=%fused_computation.8 | loop fusion | flops 18874368 | bytes 50331648 | tf_op jit(solution)/shard_map/convert_element_type | solution.py:153
  (11 shorter events, 0.1 us)
Async XLA Ops:
  0.6 93.9 %copy-start = (f32[4]{0:T(128)S(1)}, f32[4]{0:T(128)}, u32[]{:S(2)}) copy-start(f32[4]{0:T(128)} %param.17) | copy-start | bytes 52
  5.5 20.5 %all-to-all-start = ((s32[128,1,1,16]{3,2,1,0:T(1,128)}), s32[128,1,1,16]{3,2,1,0:T(1,128)S(1)}, u32[]{:S(2)}, u32[]{:S(2)}) async-start(s32[128,1,1,16]{3,2,1,0:T(1,128)} %bitcast.2), calls=%async_computation | async-start | bytes 131072 | tf_op jit(solution)/shard_map/all_to_all | solution.py:26
  26.0 18.3 %all-to-all-start.1 = ((bf16[128,1,1,16,128]{4,3,2,1,0:T(8,128)(2,1)}), bf16[128,1,1,16,128]{4,3,2,1,0:T(8,128)(2,1)S(1)}, u32[]{:S(2)}, u32[]{:S(2)}) async-start(bf16[128,1,1,16,128]{4,3,2,1,0:T(8,128)(2,1)} %bitcast.9), calls=%async_computation.1 | async-start | bytes 1048576 | tf_op jit(solution)/shard_map/all_to_all | solution.py:26
  52.0 9.3 %all-to-all-start.2 = ((f32[4,32,256]{2,1,0:T(8,128)}), f32[4,32,256]{2,1,0:T(8,128)S(1)}, u32[]{:S(2)}, u32[]{:S(2)}) async-start(f32[4,32,256]{2,1,0:T(8,128)} %bitcast.15), calls=%async_computation.2 | async-start | bytes 262144 | tf_op jit(solution)/shard_map/all_to_all | solution.py:118
  83.4 12.4 %all-to-all-start.4 = ((f32[4,32,256]{2,1,0:T(8,128)}), f32[4,32,256]{2,1,0:T(8,128)S(1)}, u32[]{:S(2)}, u32[]{:S(2)}) async-start(f32[4,32,256]{2,1,0:T(8,128)} %broadcast_in_dim.23), calls=%async_computation.4 | async-start | bytes 262144 | tf_op jit(solution)/shard_map/all_to_all | solution.py:39
  120.2 10.6 %all-to-all-start.5 = ((bf16[4,1,128,128]{2,3,1,0:T(8,128)(2,1)}), bf16[4,1,128,128]{2,3,1,0:T(8,128)(2,1)S(1)}, u32[]{:S(2)}, u32[]{:S(2)}) async-start(bf16[4,1,128,128]{2,3,1,0:T(8,128)(2,1)} %broadcast_in_dim.24), calls=%async_computation.5 | async-start | bytes 262144 | tf_op jit(solution)/shard_map/all_to_all | solution.py:39
where the time goes:
time: 190 us; the launch traced here: 189 us
  other arithmetic  57.1 us (30%)
  matrix products  42.1 us (22%)
  waiting for transfers between devices  30.7 us (16%)
  starting transfers between devices  27.4 us (14%)
  blocking collectives  20.9 us (11%)
  local copies, waits for them, and re-layouts  8.49 us (4%)
  between operations  2.19 us (1%)
    dot_general x1, matrix products, on_device(): jnp.dot(anomalies, joined_transforms, preferred_element_type=jnp.float32)  40.6 us
    all_to_all x1, blocking collectives, summed_on_arrival(): lax.all_to_all(cut_along(array, dim, devices), axis, 0, 0, tiled=True)  20.9 us
    all_to_all x2, waiting for transfers between devices, exchange_both(): lax.all_to_all(blocks, axis, split_axis=0, concat_axis=0, tiled=True)  19 us
    convert_element_type x1, other arithmetic, on_device(): updated = (field + change[:, 0, :]).astype(jnp.bfloat16)  17.4 us
    all_to_all x2, starting transfers between devices, exchange_both(): lax.all_to_all(blocks, axis, split_axis=0, concat_axis=0, tiled=True)  16 us
    another operation x3, other arithmetic, solve_lambdas(): factor = jnp.linalg.cholesky(systems)  12.4 us
    another operation x2, other arithmetic, solve_lambdas(): jax.scipy.linalg.cho_solve((factor, True), targets).astype(jnp.bfloat16)  10.5 us
    all_to_all x2, starting transfers between devices, sent_to_all(): return lax.all_to_all(copies, axis, split_axis=0, concat_axis=0, tiled=True)  8.08 us
  transfers between devices with their start and end apart: 5, of which 4 were waited for; matrix products, arithmetic and copies ran while one was open for 6% of the time, Pallas kernels for 0%

commit v1 on v0

v1 whole, which is shorter than its diff:
```python
import jax
import jax.numpy as jnp
from jax import lax
from jax.experimental import pallas as pl
from jax.experimental.pallas import tpu as pltpu
from jax.sharding import PartitionSpec as P

CAP = 16
EXTRA = 8
F32 = jnp.float32
BF16 = jnp.bfloat16
HIGHEST = lax.Precision.HIGHEST
SMEM = pl.BlockSpec(memory_space=pltpu.SMEM)
VMEM = pl.BlockSpec(memory_space=pltpu.VMEM)
MIB = 1 << 20


def iota(shape, dim):
    return lax.broadcasted_iota(jnp.int32, shape, dim)


def one_hot(cond):
    return jnp.where(cond, 1.0, 0.0).astype(BF16)


def dot(a, b, contract=((1,), (0,)), precision=None):
    return lax.dot_general(
        a, b, (contract, ((), ())), precision=precision, preferred_element_type=F32
    )


def params(mib):
    return pltpu.CompilerParams(vmem_limit_bytes=mib * MIB)


def cost(flops, size):
    return pl.CostEstimate(flops=int(flops), bytes_accessed=int(size), transcendentals=0)


def send_rows(slot_well, tile_count, heads, n_obs, n_cell, wells_dev):
    slots, members = heads.shape
    rows = n_obs * CAP

    def body(count_ref, well_ref, heads_ref, out_ref):
        well = well_ref[...]
        valid = iota((1, slots), 1) < count_ref[0]
        block = jnp.where(valid, well // wells_dev, -1)
        place = well % wells_dev
        hits = one_hot(iota((n_obs * n_cell, slots), 0) == block)
        before = one_hot(iota((slots, slots), 0) < iota((slots, slots), 1))
        rank = jnp.sum(dot(hits, before) * hits.astype(F32), axis=0, keepdims=True)
        row = (block // n_cell) * CAP + rank.astype(jnp.int32)
        column = jnp.where(valid, block % n_cell, -1)
        target = jnp.where(valid, column * rows + row, -1)
        marks = jnp.where(iota((n_cell, slots), 0) == column, place + 1, 0)
        marks = marks.astype(F32).astype(BF16)
        places = dot(marks, one_hot(iota((members, slots), 0) == row), ((1,), (1,)))
        values = heads_ref[...]
        for c in range(n_cell):
            pick = one_hot(iota((rows, slots), 0) + c * rows == target)
            out_ref[c, 0:rows, :] = dot(pick, values).astype(BF16)
            out_ref[c, rows : rows + EXTRA, :] = jnp.broadcast_to(
                places[c : c + 1, :], (EXTRA, members)
            ).astype(BF16)

    return pl.pallas_call(
        body,
        out_shape=jax.ShapeDtypeStruct((n_cell, rows + EXTRA, members), BF16),
        in_specs=[SMEM, VMEM, VMEM],
        out_specs=VMEM,
        compiler_params=params(16),
        cost_estimate=cost(1e9, 1e6),
        name="send_rows",
    )(tile_count, slot_well.reshape(1, slots), heads)


def block_grams(place_obs, received, wells, n_obs):
    sources, height, members = received.shape
    rows = n_obs * CAP
    slots = sources * CAP
    wells_dev = wells[0].shape[0] - EXTRA
    band = members // n_obs

    def body(me_ref, recv_ref, *refs):
        well_refs, out_refs, gram_ref = refs[:n_obs], refs[n_obs : 2 * n_obs], refs[-1]
        me = me_ref[0]
        tail = recv_ref[:, rows : rows + EXTRA, :].astype(F32)
        places = jnp.max(tail, axis=1).astype(BF16)
        mine = iota((sources, slots), 0) == iota((sources, slots), 1) // CAP
        eye = iota((wells_dev, wells_dev), 0) == iota((wells_dev, wells_dev), 1)
        for k in range(n_obs):
            owner = lax.rem(me - k + n_obs, n_obs)
            first = owner * CAP
            spread = one_hot(
                iota((members, slots), 0) == iota((members, slots), 1) % CAP + first
            )
            spot = jnp.where(mine, dot(places, spread), 0.0)
            spot = jnp.sum(spot, axis=0, keepdims=True).astype(jnp.int32)
            pick = one_hot(iota((wells_dev, slots), 0) + 1 == spot)
            heads = recv_ref[:, pl.ds(pl.multiple_of(first, CAP), CAP), :]
            predicted = dot(pick, heads.reshape(slots, members))
            mean = jnp.sum(predicted, axis=1, keepdims=True) * (1.0 / members)
            deviation = well_refs[k][wells_dev : wells_dev + 1, :]
            deviation = jnp.sum(jnp.where(eye, deviation, 0.0), axis=1, keepdims=True)
            scale = 1.0 / deviation
            scaled = (predicted - mean) * scale
            innovation = (well_refs[k][0:wells_dev, :] - predicted) * scale
            joined = jnp.concatenate([scaled, innovation], axis=1)
            gram_ref[...] = dot(scaled.T, joined, precision=HIGHEST)
            for step in range(n_obs):
                dest = lax.rem(me + step, n_obs)
                part = gram_ref[pl.ds(pl.multiple_of(dest * band, band), band), :]
                out_refs[step][owner] = part.astype(BF16)

    return pl.pallas_call(
        body,
        out_shape=[jax.ShapeDtypeStruct((n_obs, band, 2 * members), BF16)] * n_obs,
        in_specs=[SMEM] + [VMEM] * (1 + n_obs),
        out_specs=[VMEM] * n_obs,
        scratch_shapes=[pltpu.VMEM((members, 2 * members), F32)],
        compiler_params=params(16),
        cost_estimate=cost(1e9, 1e6),
        name="block_grams",
    )(place_obs, received, *wells)


def tile_terms(weights, parts):
    n_tiles, n_obs = weights.shape
    _, band, width = parts[0].shape

    def body(weight_ref, *refs):
        out_ref = refs[-1]
        totals = []
        for o in range(n_obs):
            total = refs[0][o].astype(F32)
            for ref in refs[1:-1]:
                total = total + ref[o].astype(F32)
            totals.append(total)
        for t in range(n_tiles):
            term = weight_ref[t, 0] * totals[0]
            for o in range(1, n_obs):
                term = term + weight_ref[t, o] * totals[o]
            out_ref[t] = term.astype(BF16)

    return pl.pallas_call(
        body,
        out_shape=jax.ShapeDtypeStruct((n_tiles, band, width), BF16),
        in_specs=[SMEM] + [VMEM] * len(parts),
        out_specs=VMEM,
        compiler_params=params(16),
        cost_estimate=cost(1e8, 1e6),
        name="tile_terms",
    )(weights, *parts)


def invert_packed(packed, size, groups):
    lanes = size * groups
    lane = iota((size, lanes), 1)
    row = iota((size, lanes), 0)
    for j in range(size):
        column = jnp.take_along_axis(
            packed, lane // size * size + j, axis=1, mode="promise_in_bounds"
        )
        inverse = 1.0 / column[j : j + 1, :]
        pivot_row = packed[j : j + 1, :] * inverse
        here = lane % size == j
        others = jnp.where(here, -(column * inverse), packed - column * pivot_row)
        packed = jnp.where(row == j, jnp.where(here, inverse, pivot_row), others)
    return packed


def solve_all(place_obs, lambdas, bands, field_gram):
    n_obs = len(bands)
    band, width = bands[0].shape
    members = width // 2
    n_lam = lambdas.shape[0]
    size = members // n_lam

    def body(me_ref, lam_ref, *refs):
        band_refs = refs[:n_obs]
        gram_ref, out_ref, norm_ref, full_ref, work_ref = refs[n_obs:]
        me = me_ref[0]
        for k in range(n_obs):
            owner = lax.rem(me - k + n_obs, n_obs)
            full_ref[pl.ds(pl.multiple_of(owner * band, band), band), :] = band_refs[k][...]
        full = full_ref[...]
        diagonal = iota((members, width), 0) == iota((members, width), 1)
        for l in range(n_lam):
            shift = (1.0 + lam_ref[l]) * (members - 1)
            work_ref[l] = full + jnp.where(diagonal, shift, 0.0)
        lane = iota((size, members), 1)
        tall_lane = iota((members, members), 1)
        tall_row = iota((members, width), 0)
        for kb in range(members // size):
            at = kb * size
            packed = jnp.zeros((size, members), F32)
            for l in range(n_lam):
                piece = work_ref[l, at : at + size, 0:members]
                turn = (l - kb) * size % members
                piece = pltpu.roll(piece, turn, 1) if turn else piece
                packed = jnp.where(lane // size == l, piece, packed)
            packed = invert_packed(packed, size, n_lam)
            diag = jnp.concatenate(
                [jnp.where(lane // size == l, packed, 0.0) for l in range(n_lam)], axis=0
            )
            rows = jnp.concatenate(
                [work_ref[l, at : at + size, :] for l in range(n_lam)], axis=0
            )
            upper = dot(diag, rows, precision=HIGHEST)
            left = []
            for l in range(n_lam):
                piece = work_ref[l, :, 0:members]
                turn = (l - kb) * size % members
                piece = pltpu.roll(piece, turn, 1) if turn else piece
                left.append(jnp.where(tall_lane // size == l, piece, 0.0))
            delta = dot(jnp.concatenate(left, axis=0), upper, precision=HIGHEST)
            for l in range(n_lam):
                work_ref[l] = work_ref[l] - delta[l * members : (l + 1) * members, :]
                work_ref[l, at : at + size, :] = upper[l * size : (l + 1) * size, :]
        for l in range(n_lam):
            transform = work_ref[l, :, members:width].astype(BF16).astype(F32)
            spread = dot(gram_ref[...], transform, precision=HIGHEST)
            norm_ref[l : l + 1, :] = jnp.sum(transform * spread, axis=0, keepdims=True)
            if l == 0:
                mean = jnp.sum(transform, axis=0, keepdims=True) * (1.0 / members)
                centred = transform - mean
                high = centred.astype(BF16)
                out_ref[0:members, :] = high
                out_ref[members:width, :] = (centred - high.astype(F32)).astype(BF16)

    return pl.pallas_call(
        body,
        out_shape=[
            jax.ShapeDtypeStruct((width, members), BF16),
            jax.ShapeDtypeStruct((n_lam, members), F32),
        ],
        in_specs=[SMEM, SMEM] + [VMEM] * (n_obs + 1),
        out_specs=[VMEM, VMEM],
        scratch_shapes=[
            pltpu.VMEM((members, width), F32),
            pltpu.VMEM((n_lam, members, width), F32),
        ],
        compiler_params=params(16),
        cost_estimate=cost(1e9, 1e6),
        name="solve_all",
    )(place_obs, lambdas, *bands, field_gram)


def field_moments(log_k, start, count, chunk):
    members = log_k.shape[1]
    first = start // chunk

    def body(x_ref, out_ref):
        x = x_ref[...]
        spread = jnp.full((members, members), 1.0 / members, BF16)
        anomalies = (x.astype(F32) - dot(x, spread)).astype(BF16)
        part = dot(anomalies, anomalies, ((0,), (0,)))

        @pl.when(pl.program_id(0) == 0)
        def _():
            out_ref[...] = part

        @pl.when(pl.program_id(0) > 0)
        def _():
            out_ref[...] += part

    return pl.pallas_call(
        body,
        grid=(count // chunk,),
        out_shape=jax.ShapeDtypeStruct((members, members), F32),
        in_specs=[pl.BlockSpec((chunk, members), lambda i: (i + first, 0))],
        out_specs=pl.BlockSpec((members, members), lambda i: (0, 0)),
        compiler_params=params(16),
        cost_estimate=cost(6.0e9, count * members * 2),
        name="field_moments",
    )(log_k)


def update_field(log_k, transform, chunk):
    cells, members = log_k.shape

    def body(x_ref, t_ref, out_ref):
        x = x_ref[...]
        change = dot(jnp.concatenate([x, x], axis=1), t_ref[...])
        out_ref[...] = (x.astype(F32) + change).astype(BF16)

    return pl.pallas_call(
        body,
        grid=(cells // chunk,),
        out_shape=jax.ShapeDtypeStruct((cells, members), BF16),
        in_specs=[
            pl.BlockSpec((chunk, members), lambda i: (i, 0)),
            pl.BlockSpec((2 * members, members), lambda i: (0, 0)),
        ],
        out_specs=pl.BlockSpec((chunk, members), lambda i: (i, 0)),
        compiler_params=params(32),
        cost_estimate=cost(4 * cells * members * members, 4 * cells * members),
        name="update_field",
    )(log_k, transform)


def shifted(array, axis, step):
    n = lax.axis_size(axis)
    return lax.ppermute(array, axis, [(i, (i + step) % n) for i in range(n)])


def on_device(
    log_k, heads_pred, slot_well, tile_count, obs_values, obs_std, loc_blocks, taper, lambdas
):
    n_obs = lax.axis_size("obs")
    n_cell = lax.axis_size("cell")
    wells_dev, members = obs_values.shape
    place_obs = lax.axis_index("obs").astype(jnp.int32).reshape(1)
    sent = send_rows(slot_well, tile_count, heads_pred, n_obs, n_cell, wells_dev)
    received = lax.all_to_all(sent, "cell", split_axis=0, concat_axis=0, tiled=True)
    own_wells = jnp.concatenate(
        [obs_values, jnp.broadcast_to(obs_std[None], (EXTRA, wells_dev))], axis=0
    )
    wells = [own_wells] + [shifted(own_wells, "obs", k) for k in range(1, n_obs)]
    cells = log_k.shape[0]
    gram_a = field_moments(log_k, 0, cells // 2, 2048)
    gram_b = field_moments(log_k, cells // 2, cells // 2, 2048)
    column_blocks = jnp.arange(n_obs, dtype=jnp.int32) * n_cell + lax.axis_index("cell")
    weights = jnp.sum(
        taper[:, :, None]
        * (loc_blocks[:, :, None] == column_blocks[None, None, :]).astype(F32),
        axis=1,
    )
    grams = block_grams(place_obs, received, wells, n_obs)
    parts = [grams[0]] + [shifted(grams[k], "obs", k) for k in range(1, n_obs)]
    terms = tile_terms(weights, parts)
    gathered = lax.all_to_all(terms, "cell", split_axis=0, concat_axis=0, tiled=True)
    own_band = jnp.sum(gathered.astype(F32), axis=0)
    bands = [own_band] + [shifted(own_band, "obs", k) for k in range(1, n_obs)]
    transform, norms = solve_all(place_obs, lambdas, bands, gram_a + gram_b)
    return (update_field(log_k, transform, 4096), norms[None])


def solution(mesh):
    return jax.shard_map(
        on_device,
        mesh=mesh,
        in_specs=(
            P(("obs", "cell"), None),
            P(("obs", "cell"), None),
            P(("obs", "cell")),
            P(("obs", "cell")),
            P(("obs", "cell"), None),
            P(("obs", "cell")),
            P(),
            P(),
            P(),
        ),
        out_specs=(P(("obs", "cell"), None), P(("obs", "cell"), None, None)),
        check_vma=False,
    )
```

time: 190 us -> 99.9 us (0.53)
  other arithmetic: 57.1 us -> 1.73 us
  Pallas kernels: 0 us -> 48.1 us
  matrix products: 42.1 us -> 0 us
  waiting for transfers between devices: 30.7 us -> 8.23 us
  blocking collectives: 20.9 us -> 0 us
  local copies, waits for them, and re-layouts: 8.49 us -> 11.5 us
    pallas_call x0 -> x7, Pallas kernels: none -> 48.1 us  [the longest x1 17.5 us: solve_all(): pl.pallas_call(body, out_shape=[jax.ShapeDtypeStruct((width, members), BF...]
    dot_general x2 -> x0, matrix products: 41.6 us -> none  [the longest x1 40.6 us: on_device(): jnp.dot(anomalies, joined_transforms, preferred_element_type=jnp.float32)]
    all_to_all x5 -> x2, waiting for transfers between devices: 30.7 us -> 0.72 us  [the longest x1 0.72 us: on_device(): lax.all_to_all(sent, 'cell', split_axis=0, concat_axis=0, tiled=True)]
    another operation x5 -> x0, other arithmetic: 22.9 us -> none  [the longest x3 12.4 us: solve_lambdas(): factor = jnp.linalg.cholesky(systems)]
    all_to_all x1 -> x0, blocking collectives: 20.9 us -> none  [summed_on_arrival(): lax.all_to_all(cut_along(array, dim, devices), axis, 0, 0, tiled=True)]
    convert_element_type x2 -> x0, other arithmetic: 17.4 us -> none  [the longest x1 17.4 us: on_device(): updated = (field + change[:, 0, :]).astype(jnp.bfloat16)]
    all_to_all x5 -> x2, starting transfers between devices: 27.4 us -> 13.1 us  [the longest x1 8.28 us: on_device(): lax.all_to_all(sent, 'cell', split_axis=0, concat_axis=0, tiled=True)]
    ppermute x0 -> x9, starting transfers between devices: none -> 14.2 us  [shifted(): return lax.ppermute(array, axis, [(i, (i + step) % n) for i in range(n)])]
  transfers between devices with their start and end apart: 5 -> 11, of which waited for: 4 -> 6; matrix products, arithmetic and copies ran while one was open for 6% -> 2% of each run, Pallas kernels for 0% -> 15%
where the time goes in v1:
time: 99.9 us; the launch traced here: 98.2 us
  Pallas kernels  48.1 us (48%)
  starting transfers between devices  27.3 us (27%)
  local copies, waits for them, and re-layouts  11.5 us (12%)
  waiting for transfers between devices  8.23 us (8%)
  other arithmetic  1.73 us (2%)
  between operations  1.41 us (1%)
    pallas_call x1, Pallas kernels, solve_all(): pl.pallas_call(body, out_shape=[jax.ShapeDtypeStruct((width, members), BF...  17.5 us
    pallas_call x2, Pallas kernels, field_moments(): pl.pallas_call(body, grid=(count // chunk,), out_shape=jax.ShapeDtypeStru...  14.5 us
    ppermute x9, starting transfers between devices, shifted(): return lax.ppermute(array, axis, [(i, (i + step) % n) for i in range(n)])  14.2 us
    pallas_call x1, Pallas kernels, update_field(): pl.pallas_call(body, grid=(cells // chunk,), out_shape=jax.ShapeDtypeStru...  10.8 us
    unnamed x12, local copies, waits for them, and re-layouts  10.7 us
    all_to_all x1, starting transfers between devices, on_device(): lax.all_to_all(sent, 'cell', split_axis=0, concat_axis=0, tiled=True)  8.28 us
    ppermute x9, waiting for transfers between devices, shifted(): return lax.ppermute(array, axis, [(i, (i + step) % n) for i in range(n)])  7.51 us
    all_to_all x1, starting transfers between devices, on_device(): lax.all_to_all(terms, 'cell', split_axis=0, concat_axis=0, tiled=True)  4.81 us
  transfers between devices with their start and end apart: 11, of which 6 were waited for; matrix products, arithmetic and copies ran while one was open for 2% of the time, Pallas kernels for 15%

profile of v1, /device:TPU:0, one launch (start us, length us, event | category | flops | bytes accessed | tf_op | source)
XLA Modules:
  0.0 98.2 jit_solution(17763969609698781508)
XLA Ops:
  1.3 0.0 copy-start.3
  1.3 0.9 copy-done.3
  2.2 0.0 copy-start.4
  2.2 0.7 copy-done.4
  2.9 1.8 %send_rows.1 = bf16[32,72,128]{2,1,0:T(8,128)(2,1)} custom-call(s32[1]{0:T(128)S(6)} %copy.14.count_ref, s32[1,512]{1,0:T(1,128)S(1)} %bitcast.3, bf16[512,128]{1,0:T(8,128)(2,1)S(1)} %copy-done.3), custom_call_target="tpu_custom_call" | custom-call | flops 1000000000 | bytes 1000000 | tf_op jit(solution)/shard_map/send_rows/pallas_call | solution.py:66
  4.6 8.3 %all-to-all-start = ((bf16[32,72,128]{2,1,0:T(8,128)(2,1)}), bf16[32,72,128]{2,1,0:T(8,128)(2,1)S(1)}, u32[]{:S(2)}, u32[]{:S(2)}) async-start(bf16[32,72,128]{2,1,0:T(8,128)(2,1)} %send_rows.1), calls=%async_computation | async-start | bytes 1179648 | tf_op jit(solution)/shard_map/all_to_all | solution.py:315
  12.9 0.7 broadcast_in_dim.4
  13.6 0.8 pad_maximum_fusion.refs_0_
  14.4 3.0 %collective-permute-start.2 = (f32[136,128]{1,0:T(8,128)S(1)}, f32[136,128]{1,0:T(8,128)S(1)}, u32[]{:S(2)}, u32[]{:S(2)}) collective-permute-start(f32[136,128]{1,0:T(8,128)S(1)} %pad_maximum_fusion.refs_0_), channel_id=1, source_target_pairs={{0,96},{32,0},{64,32},{96,64},{1,97},{33,1},{65,33},{97,65},{2,98}... | collective-permute-start | bytes 208904 | tf_op jit(solution)/shard_map/ppermute | solution.py:304
  17.4 0.6 collective-permute-start.1
  18.1 1.0 collective-permute-start
  19.1 1.8 %collective-permute-done.2.refs_3_ = f32[136,128]{1,0:T(8,128)S(1)} collective-permute-done((f32[136,128]{1,0:T(8,128)S(1)}, f32[136,128]{1,0:T(8,128)S(1)}, u32[]{:S(2)}, u32[]{:S(2)}) %collective-permute-start.2) | collective-permute-done | bytes 69664 | tf_op jit(solution)/shard_map/ppermute | solution.py:304
  20.9 2.9 %collective-permute-done.1.refs_2_ = f32[136,128]{1,0:T(8,128)S(1)} collective-permute-done((f32[136,128]{1,0:T(8,128)S(1)}, f32[136,128]{1,0:T(8,128)S(1)}, u32[]{:S(2)}, u32[]{:S(2)}) %collective-permute-start.1) | collective-permute-done | bytes 69664 | tf_op jit(solution)/shard_map/ppermute | solution.py:304
  23.8 0.7 collective-permute-done.refs_1_
  24.5 0.7 all-to-all-done.recv_ref
  25.2 1.6 %block_grams.1 = (bf16[4,32,256]{2,1,0:T(8,128)(2,1)S(1)}, bf16[4,32,256]{2,1,0:T(8,128)(2,1)S(1)}, bf16[4,32,256]{2,1,0:T(8,128)(2,1)S(1)}, bf16[4,32,256]{2,1,0:T(8,128)(2,1)S(1)}) custom-call(s32[1]{0:T(128)} %bitcast.me_ref, bf16[32,72,128]{2,1,0:T(8,128)(2,1)S(1)} %all-to-all-done.recv_ref, f32[136,128]{1,0:T(8,128)S(1)} %pad_maximum_fusion.refs_0_, ...), custom_call_target="tpu_custom_call" | custom-call | flops 1000000000 | bytes 1000000 | tf_op jit(solution)/shard_map/block_grams/pallas_call | solution.py:115
  26.9 1.7 %collective-permute-start.3 = (bf16[4,32,256]{2,1,0:T(8,128)(2,1)S(1)}, bf16[4,32,256]{2,1,0:T(8,128)(2,1)S(1)}, u32[]{:S(2)}, u32[]{:S(2)}) collective-permute-start(bf16[4,32,256]{2,1,0:T(8,128)(2,1)S(1)} %get-tuple-element.9), channel_id=1, source_target_pairs={{0,32},{32,64},{64,96},{96,0},{1,33},{33,65},{65,97},{97,1},{2,34}... | collective-permute-start | bytes 196616 | tf_op jit(solution)/shard_map/ppermute | solution.py:304
  28.5 2.9 %collective-permute-start.4 = (bf16[4,32,256]{2,1,0:T(8,128)(2,1)S(1)}, bf16[4,32,256]{2,1,0:T(8,128)(2,1)S(1)}, u32[]{:S(2)}, u32[]{:S(2)}) collective-permute-start(bf16[4,32,256]{2,1,0:T(8,128)(2,1)S(1)} %get-tuple-element.10), channel_id=1, source_target_pairs={{0,64},{32,96},{64,0},{96,32},{1,65},{33,97},{65,1},{97,33},{2,66}... | collective-permute-start | bytes 196616 | tf_op jit(solution)/shard_map/ppermute | solution.py:304
  31.4 1.4 %collective-permute-start.5 = (bf16[4,32,256]{2,1,0:T(8,128)(2,1)S(1)}, bf16[4,32,256]{2,1,0:T(8,128)(2,1)S(1)}, u32[]{:S(2)}, u32[]{:S(2)}) collective-permute-start(bf16[4,32,256]{2,1,0:T(8,128)(2,1)S(1)} %get-tuple-element.11), channel_id=1, source_target_pairs={{0,96},{32,0},{64,32},{96,64},{1,97},{33,1},{65,33},{97,65},{2,98}... | collective-permute-start | bytes 196616 | tf_op jit(solution)/shard_map/ppermute | solution.py:304
  32.8 0.8 select_reduce_fusion
  33.6 0.1 copy.13.weight_ref
  33.6 0.0 collective-permute-done.3.refs_1_
  33.7 1.2 %collective-permute-done.4.refs_2_ = bf16[4,32,256]{2,1,0:T(8,128)(2,1)S(1)} collective-permute-done((bf16[4,32,256]{2,1,0:T(8,128)(2,1)S(1)}, bf16[4,32,256]{2,1,0:T(8,128)(2,1)S(1)}, u32[]{:S(2)}, u32[]{:S(2)}) %collective-permute-start.4) | collective-permute-done | bytes 65568 | tf_op jit(solution)/shard_map/ppermute | solution.py:304
  34.9 0.8 collective-permute-done.5.refs_3_
  35.7 1.9 %tile_terms.1 = bf16[32,32,256]{2,1,0:T(8,128)(2,1)} custom-call(f32[32,4]{1,0:T(8,128)S(1)} %copy.13.weight_ref, bf16[4,32,256]{2,1,0:T(8,128)(2,1)S(1)} %get-tuple-element.8.refs_0_, bf16[4,32,256]{2,1,0:T(8,128)(2,1)S(1)} %collective-permute-done.3.refs_1_, bf16[4,32,256]{2,1,0:T(8,128)(2,1)S(1)} %collective-permute-done.4.refs_2_, ...), custom_call_target="tpu_custom_call" | custom-call | flops 100000000 | bytes 1000000 | tf_op jit(solution)/shard_map/tile_terms/pallas_call | solution.py:145
  37.6 4.8 %all-to-all-start.1 = ((bf16[32,32,256]{2,1,0:T(8,128)(2,1)}), bf16[32,32,256]{2,1,0:T(8,128)(2,1)S(1)}, u32[]{:S(2)}, u32[]{:S(2)}) async-start(bf16[32,32,256]{2,1,0:T(8,128)(2,1)} %tile_terms.1), calls=%async_computation.1 | async-start | bytes 1048576 | tf_op jit(solution)/shard_map/all_to_all | solution.py:332
  42.4 0.0 copy-start
  42.4 4.6 %copy-done = bf16[49152,128]{1,0:T(8,128)(2,1)S(1)} copy-done((bf16[49152,128]{1,0:T(8,128)(2,1)S(1)}, bf16[49152,128]{1,0:T(8,128)(2,1)}, u32[]{:S(2)}) %copy-start) | copy-done | bytes 12582936
  47.0 7.3 %field_moments.2 = f32[128,128]{1,0:T(8,128)S(1)} custom-call(bf16[49152,128]{1,0:T(8,128)(2,1)S(1)} %copy-done), custom_call_target="tpu_custom_call" | custom-call | flops 6000000000 | bytes 6291456 | tf_op jit(solution)/shard_map/field_moments/pallas_call | solution.py:267
  54.2 0.0 copy-start.5
  54.3 0.0 all-to-all-done.1
  54.3 0.1 convert_reduce_fusion.refs_0_
  54.4 2.7 %collective-permute-start.8 = (f32[32,256]{1,0:T(8,128)S(1)}, f32[32,256]{1,0:T(8,128)S(1)}, u32[]{:S(2)}, u32[]{:S(2)}) collective-permute-start(f32[32,256]{1,0:T(8,128)S(1)} %convert_reduce_fusion.refs_0_), channel_id=1, source_target_pairs={{0,96},{32,0},{64,32},{96,64},{1,97},{33,1},{65,33},{97,65},{2,98}... | collective-permute-start | bytes 98312 | tf_op jit(solution)/shard_map/ppermute | solution.py:304
  57.1 0.7 collective-permute-start.7
  57.8 0.2 collective-permute-start.6
  58.0 0.0 copy-start.1
  58.0 4.6 %copy-done.1 = bf16[49152,128]{1,0:T(8,128)(2,1)S(1)} copy-done((bf16[49152,128]{1,0:T(8,128)(2,1)S(1)}, bf16[49152,128]{1,0:T(8,128)(2,1)}, u32[]{:S(2)}) %copy-start.1) | copy-done | bytes 12582936
  62.6 0.0 copy-start.2
  62.6 7.3 %field_moments.3 = f32[128,128]{1,0:T(8,128)S(1)} custom-call(bf16[49152,128]{1,0:T(8,128)(2,1)S(1)} %copy-done.1), custom_call_target="tpu_custom_call" | custom-call | flops 6000000000 | bytes 6291456 | tf_op jit(solution)/shard_map/field_moments/pallas_call | solution.py:267
  69.9 0.0 collective-permute-done.8.refs_3_
  69.9 0.0 collective-permute-done.7.refs_2_
  69.9 0.0 collective-permute-done.6.refs_1_
  69.9 0.0 copy-done.5
  69.9 17.5 %solve_all.1 = (bf16[256,128]{1,0:T(8,128)(2,1)S(1)}, f32[4,128]{1,0:T(4,128)}) custom-call(s32[1]{0:T(128)} %bitcast.me_ref, f32[4]{0:T(128)S(1)} %copy-done.5, f32[32,256]{1,0:T(8,128)S(1)} %convert_reduce_fusion.refs_0_, f32[32,256]{1,0:T(8,128)S(1)} %collective-permute-done.6.refs_1_, f32[32,256]{1,0:T(8,128)S(1)} %collective-permute-done.7.refs_2_, ...), custom_call_target="tpu_custom_call" | custom-call | flops 1000000000 | bytes 1000000 | tf_op jit(solution)/shard_map/solve_all/pallas_call | solution.py:231
  87.5 0.0 copy-done.2
  87.5 10.8 %update_field.1 = bf16[49152,128]{1,0:T(8,128)(2,1)} custom-call(bf16[49152,128]{1,0:T(8,128)(2,1)S(1)} %copy-done.2, bf16[256,128]{1,0:T(8,128)(2,1)S(1)} %get-tuple-element.12.t_ref), custom_call_target="tpu_custom_call" | custom-call | flops 3221225472 | bytes 25165824 | tf_op jit(solution)/shard_map/update_field/pallas_call | solution.py:287
  (2 shorter events, 0.0 us)
Async XLA Ops:
  1.3 0.9 copy-start.3
  2.2 0.7 copy-start.4
  4.6 20.6 %all-to-all-start = ((bf16[32,72,128]{2,1,0:T(8,128)(2,1)}), bf16[32,72,128]{2,1,0:T(8,128)(2,1)S(1)}, u32[]{:S(2)}, u32[]{:S(2)}) async-start(bf16[32,72,128]{2,1,0:T(8,128)(2,1)} %send_rows.1), calls=%async_computation | async-start | bytes 1179648 | tf_op jit(solution)/shard_map/all_to_all | solution.py:315
  14.4 6.4 %collective-permute-start.2 = (f32[136,128]{1,0:T(8,128)S(1)}, f32[136,128]{1,0:T(8,128)S(1)}, u32[]{:S(2)}, u32[]{:S(2)}) collective-permute-start(f32[136,128]{1,0:T(8,128)S(1)} %pad_maximum_fusion.refs_0_), channel_id=1, source_target_pairs={{0,96},{32,0},{64,32},{96,64},{1,97},{33,1},{65,33},{97,65},{2,98}... | collective-permute-start | bytes 208904 | tf_op jit(solution)/shard_map/ppermute | solution.py:304
  17.4 6.3 %collective-permute-start.1 = (f32[136,128]{1,0:T(8,128)S(1)}, f32[136,128]{1,0:T(8,128)S(1)}, u32[]{:S(2)}, u32[]{:S(2)}) collective-permute-start(f32[136,128]{1,0:T(8,128)S(1)} %pad_maximum_fusion.refs_0_), channel_id=1, source_target_pairs={{0,64},{32,96},{64,0},{96,32},{1,65},{33,97},{65,1},{97,33},{2,66}... | collective-permute-start | bytes 208904 | tf_op jit(solution)/shard_map/ppermute | solution.py:304
  18.1 6.4 %collective-permute-start = (f32[136,128]{1,0:T(8,128)S(1)}, f32[136,128]{1,0:T(8,128)S(1)}, u32[]{:S(2)}, u32[]{:S(2)}) collective-permute-start(f32[136,128]{1,0:T(8,128)S(1)} %pad_maximum_fusion.refs_0_), channel_id=1, source_target_pairs={{0,32},{32,64},{64,96},{96,0},{1,33},{33,65},{65,97},{97,1},{2,34}... | collective-permute-start | bytes 208904 | tf_op jit(solution)/shard_map/ppermute | solution.py:304
  26.9 6.8 %collective-permute-start.3 = (bf16[4,32,256]{2,1,0:T(8,128)(2,1)S(1)}, bf16[4,32,256]{2,1,0:T(8,128)(2,1)S(1)}, u32[]{:S(2)}, u32[]{:S(2)}) collective-permute-start(bf16[4,32,256]{2,1,0:T(8,128)(2,1)S(1)} %get-tuple-element.9), channel_id=1, source_target_pairs={{0,32},{32,64},{64,96},{96,0},{1,33},{33,65},{65,97},{97,1},{2,34}... | collective-permute-start | bytes 196616 | tf_op jit(solution)/shard_map/ppermute | solution.py:304
  28.5 6.4 %collective-permute-start.4 = (bf16[4,32,256]{2,1,0:T(8,128)(2,1)S(1)}, bf16[4,32,256]{2,1,0:T(8,128)(2,1)S(1)}, u32[]{:S(2)}, u32[]{:S(2)}) collective-permute-start(bf16[4,32,256]{2,1,0:T(8,128)(2,1)S(1)} %get-tuple-element.10), channel_id=1, source_target_pairs={{0,64},{32,96},{64,0},{96,32},{1,65},{33,97},{65,1},{97,33},{2,66}... | collective-permute-start | bytes 196616 | tf_op jit(solution)/shard_map/ppermute | solution.py:304
  31.4 4.3 %collective-permute-start.5 = (bf16[4,32,256]{2,1,0:T(8,128)(2,1)S(1)}, bf16[4,32,256]{2,1,0:T(8,128)(2,1)S(1)}, u32[]{:S(2)}, u32[]{:S(2)}) collective-permute-start(bf16[4,32,256]{2,1,0:T(8,128)(2,1)S(1)} %get-tuple-element.11), channel_id=1, source_target_pairs={{0,96},{32,0},{64,32},{96,64},{1,97},{33,1},{65,33},{97,65},{2,98}... | collective-permute-start | bytes 196616 | tf_op jit(solution)/shard_map/ppermute | solution.py:304
  37.6 16.7 %all-to-all-start.1 = ((bf16[32,32,256]{2,1,0:T(8,128)(2,1)}), bf16[32,32,256]{2,1,0:T(8,128)(2,1)S(1)}, u32[]{:S(2)}, u32[]{:S(2)}) async-start(bf16[32,32,256]{2,1,0:T(8,128)(2,1)} %tile_terms.1), calls=%async_computation.1 | async-start | bytes 1048576 | tf_op jit(solution)/shard_map/all_to_all | solution.py:332
  42.4 4.6 %copy-start = (bf16[49152,128]{1,0:T(8,128)(2,1)S(1)}, bf16[49152,128]{1,0:T(8,128)(2,1)}, u32[]{:S(2)}) copy-start(bf16[49152,128]{1,0:T(8,128)(2,1)} %x_ref.5) | copy-start | bytes 37748740
  54.2 15.7 %copy-start.5 = (f32[4]{0:T(128)S(1)}, f32[4]{0:T(128)}, u32[]{:S(2)}) copy-start(f32[4]{0:T(128)} %lam_ref.1) | copy-start | bytes 52
  54.4 15.6 %collective-permute-start.8 = (f32[32,256]{1,0:T(8,128)S(1)}, f32[32,256]{1,0:T(8,128)S(1)}, u32[]{:S(2)}, u32[]{:S(2)}) collective-permute-start(f32[32,256]{1,0:T(8,128)S(1)} %convert_reduce_fusion.refs_0_), channel_id=1, source_target_pairs={{0,96},{32,0},{64,32},{96,64},{1,97},{33,1},{65,33},{97,65},{2,98}... | collective-permute-start | bytes 98312 | tf_op jit(solution)/shard_map/ppermute | solution.py:304
  57.1 12.8 %collective-permute-start.7 = (f32[32,256]{1,0:T(8,128)S(1)}, f32[32,256]{1,0:T(8,128)S(1)}, u32[]{:S(2)}, u32[]{:S(2)}) collective-permute-start(f32[32,256]{1,0:T(8,128)S(1)} %convert_reduce_fusion.refs_0_), channel_id=1, source_target_pairs={{0,64},{32,96},{64,0},{96,32},{1,65},{33,97},{65,1},{97,33},{2,66}... | collective-permute-start | bytes 98312 | tf_op jit(solution)/shard_map/ppermute | solution.py:304
  57.8 12.1 %collective-permute-start.6 = (f32[32,256]{1,0:T(8,128)S(1)}, f32[32,256]{1,0:T(8,128)S(1)}, u32[]{:S(2)}, u32[]{:S(2)}) collective-permute-start(f32[32,256]{1,0:T(8,128)S(1)} %convert_reduce_fusion.refs_0_), channel_id=1, source_target_pairs={{0,32},{32,64},{64,96},{96,0},{1,33},{33,65},{65,97},{97,1},{2,34}... | collective-permute-start | bytes 98312 | tf_op jit(solution)/shard_map/ppermute | solution.py:304
  58.0 4.6 %copy-start.1 = (bf16[49152,128]{1,0:T(8,128)(2,1)S(1)}, bf16[49152,128]{1,0:T(8,128)(2,1)}, u32[]{:S(2)}) copy-start(bf16[49152,128]{1,0:T(8,128)(2,1)} %x_ref.5) | copy-start | bytes 37748740
  62.6 24.8 %copy-start.2 = (bf16[49152,128]{1,0:T(8,128)(2,1)S(1)}, bf16[49152,128]{1,0:T(8,128)(2,1)}, u32[]{:S(2)}) copy-start(bf16[49152,128]{1,0:T(8,128)(2,1)} %x_ref.5) | copy-start | bytes 37748740

commit v2 on v1

--- a/solution.py
+++ b/solution.py
@@ -5,13 +5,16 @@
 from jax.experimental.pallas import tpu as pltpu
 from jax.sharding import PartitionSpec as P
 
+
 CAP = 16
 EXTRA = 8
+SPREAD = 16
 F32 = jnp.float32
 BF16 = jnp.bfloat16
 HIGHEST = lax.Precision.HIGHEST
 SMEM = pl.BlockSpec(memory_space=pltpu.SMEM)
 VMEM = pl.BlockSpec(memory_space=pltpu.VMEM)
+ANY = pl.BlockSpec(memory_space=pl.ANY)
 MIB = 1 << 20
 
 
@@ -37,11 +40,12 @@
     return pl.CostEstimate(flops=int(flops), bytes_accessed=int(size), transcendentals=0)
 
 
-def send_rows(slot_well, tile_count, heads, n_obs, n_cell, wells_dev):
+def send_rows(slot_well, tile_count, heads, obs_values, obs_std, n_obs, n_cell):
     slots, members = heads.shape
+    wells_dev = obs_values.shape[0]
     rows = n_obs * CAP
 
-    def body(count_ref, well_ref, heads_ref, out_ref):
+    def body(count_ref, well_ref, heads_ref, value_ref, std_ref, out_ref, join_ref):
         well = well_ref[...]
         valid = iota((1, slots), 1) < count_ref[0]
         block = jnp.where(valid, well // wells_dev, -1)
@@ -62,26 +66,31 @@
             out_ref[c, rows : rows + EXTRA, :] = jnp.broadcast_to(
                 places[c : c + 1, :], (EXTRA, members)
             ).astype(BF16)
-
-    return pl.pallas_call(
-        body,
-        out_shape=jax.ShapeDtypeStruct((n_cell, rows + EXTRA, members), BF16),
-        in_specs=[SMEM, VMEM, VMEM],
-        out_specs=VMEM,
-        compiler_params=params(16),
+        join_ref[0:wells_dev, :] = value_ref[...]
+        join_ref[wells_dev:, :] = jnp.broadcast_to(std_ref[...], (EXTRA, wells_dev))
+
+    return pl.pallas_call(
+        body,
+        out_shape=[
+            jax.ShapeDtypeStruct((n_cell, rows + EXTRA, members), BF16),
+            jax.ShapeDtypeStruct((wells_dev + EXTRA, members), F32),
+        ],
+        in_specs=[SMEM] + [VMEM] * 4,
+        out_specs=[VMEM, VMEM],
+        compiler_params=params(60),
         cost_estimate=cost(1e9, 1e6),
         name="send_rows",
-    )(tile_count, slot_well.reshape(1, slots), heads)
-
-
-def block_grams(place_obs, received, wells, n_obs):
-    sources, height, members = received.shape
+    )(tile_count, slot_well.reshape(1, slots), heads, obs_values, obs_std.reshape(1, wells_dev))
+
+
+def block_grams(place_obs, received, wells, after, n_obs):
+    sources, _, members = received.shape
     rows = n_obs * CAP
     slots = sources * CAP
     wells_dev = wells[0].shape[0] - EXTRA
     band = members // n_obs
 
-    def body(me_ref, recv_ref, *refs):
+    def body(me_ref, recv_ref, after_ref, *refs):
         well_refs, out_refs, gram_ref = refs[:n_obs], refs[n_obs : 2 * n_obs], refs[-1]
         me = me_ref[0]
         tail = recv_ref[:, rows : rows + EXTRA, :].astype(F32)
@@ -104,8 +113,8 @@
             deviation = jnp.sum(jnp.where(eye, deviation, 0.0), axis=1, keepdims=True)
             scale = 1.0 / deviation
             scaled = (predicted - mean) * scale
-            innovation = (well_refs[k][0:wells_dev, :] - predicted) * scale
-            joined = jnp.concatenate([scaled, innovation], axis=1)
+            offset = (well_refs[k][0:wells_dev, :] - mean) * scale
+            joined = jnp.concatenate([scaled, offset], axis=1)
             gram_ref[...] = dot(scaled.T, joined, precision=HIGHEST)
             for step in range(n_obs):
                 dest = lax.rem(me + step, n_obs)
@@ -115,13 +124,13 @@
     return pl.pallas_call(
         body,
         out_shape=[jax.ShapeDtypeStruct((n_obs, band, 2 * members), BF16)] * n_obs,
-        in_specs=[SMEM] + [VMEM] * (1 + n_obs),
+        in_specs=[SMEM] + [VMEM] * (2 + n_obs),
         out_specs=[VMEM] * n_obs,
         scratch_shapes=[pltpu.VMEM((members, 2 * members), F32)],
         compiler_params=params(16),
         cost_estimate=cost(1e9, 1e6),
         name="block_grams",
-    )(place_obs, received, *wells)
+    )(place_obs, received, after, *wells)
 
 
 def tile_terms(weights, parts):
@@ -169,28 +178,30 @@
     return packed
 
 
-def solve_all(place_obs, lambdas, bands, field_gram):
+def halves(a):
+    high = a.astype(BF16)
+    return high, (a - high.astype(F32)).astype(BF16)
+
+
+def finish(place_obs, lambdas, bands, field_gram, log_k, count):
     n_obs = len(bands)
     band, width = bands[0].shape
     members = width // 2
     n_lam = lambdas.shape[0]
     size = members // n_lam
-
-    def body(me_ref, lam_ref, *refs):
-        band_refs = refs[:n_obs]
-        gram_ref, out_ref, norm_ref, full_ref, work_ref = refs[n_obs:]
-        me = me_ref[0]
-        for k in range(n_obs):
-            owner = lax.rem(me - k + n_obs, n_obs)
-            full_ref[pl.ds(pl.multiple_of(owner * band, band), band), :] = band_refs[k][...]
-        full = full_ref[...]
-        diagonal = iota((members, width), 0) == iota((members, width), 1)
+    cells = log_k.shape[0]
+    chunk = cells // count
+
+    def eliminate(lam_ref, full_ref, work_ref, answer_ref):
+        eye = iota((members, members), 0) == iota((members, members), 1)
         for l in range(n_lam):
             shift = (1.0 + lam_ref[l]) * (members - 1)
-            work_ref[l] = full + jnp.where(diagonal, shift, 0.0)
+            system = full_ref[:, 0:members] + jnp.where(eye, shift, 0.0)
+            known = dot(system, answer_ref[l], precision=HIGHEST)
+            work_ref[l, :, 0:members] = system
+            work_ref[l, :, members:width] = full_ref[:, members:width] - known
         lane = iota((size, members), 1)
         tall_lane = iota((members, members), 1)
-        tall_row = iota((members, width), 0)
         for kb in range(members // size):
             at = kb * size
             packed = jnp.zeros((size, members), F32)
@@ -218,85 +229,196 @@
                 work_ref[l] = work_ref[l] - delta[l * members : (l + 1) * members, :]
                 work_ref[l, at : at + size, :] = upper[l * size : (l + 1) * size, :]
         for l in range(n_lam):
-            transform = work_ref[l, :, members:width].astype(BF16).astype(F32)
-            spread = dot(gram_ref[...], transform, precision=HIGHEST)
-            norm_ref[l : l + 1, :] = jnp.sum(transform * spread, axis=0, keepdims=True)
-            if l == 0:
-                mean = jnp.sum(transform, axis=0, keepdims=True) * (1.0 / members)
-                centred = transform - mean
-                high = centred.astype(BF16)
-                out_ref[0:members, :] = high
-                out_ref[members:width, :] = (centred - high.astype(F32)).astype(BF16)
+            answer_ref[l] = answer_ref[l] + work_ref[l, :, members:width]
+
+    def body(me_ref, lam_ref, *refs):
+        band_refs = refs[:n_obs]
+        gram_ref, field_ref, out_ref, norm_ref = refs[n_obs : n_obs + 4]
+        full_ref, work_ref, power_ref, inverse_ref, answer_ref = refs[n_obs + 4 : n_obs + 9]
+        hold_ref, in_sem, out_sem = refs[n_obs + 9 :]
+        loads, stores = [], []
+        for i in range(count):
+            rows = pl.ds(i * chunk, chunk)
+            loads.append(pltpu.make_async_copy(field_ref.at[rows], hold_ref.at[i], in_sem.at[i]))
+            stores.append(pltpu.make_async_copy(hold_ref.at[i], out_ref.at[rows], out_sem.at[i]))
+            loads[i].start()
+        me = me_ref[0]
+        for k in range(n_obs):
+            owner = lax.rem(me - k + n_obs, n_obs)
+            full_ref[pl.ds(pl.multiple_of(owner * band, band), band), :] = band_refs[k][...]
+        curvature = full_ref[:, 0:members]
+        right = full_ref[:, members:width] - curvature
+        share = 1.0 / members
+        right = right - jnp.sum(right, axis=0, keepdims=True) * share
+        curvature = curvature - jnp.sum(curvature, axis=0, keepdims=True) * share
+        curvature = curvature - jnp.sum(curvature, axis=1, keepdims=True) * share
+        full_ref[:, 0:members] = curvature
+        full_ref[:, members:width] = right
+        eye = iota((members, members), 0) == iota((members, members), 1)
+        bound = jnp.max(jnp.sum(jnp.abs(curvature), axis=0, keepdims=True))
+        shifts = [(1.0 + lam_ref[l]) * (members - 1) for l in range(n_lam)]
+        least = shifts[0]
+        for shift in shifts[1:]:
+            least = jnp.minimum(least, shift)
+        rate = bound / (bound + 2.0 * least)
+        for l in range(n_lam):
+            alpha = 2.0 / (bound + 2.0 * shifts[l])
+            rest = jnp.where(eye, 1.0 - alpha * shifts[l], 0.0) - alpha * curvature
+            inverse_ref[l] = alpha * (jnp.where(eye, 1.0, 0.0) + rest)
+            rest = rest.astype(BF16)
+            power_ref[l] = dot(rest, rest).astype(BF16)
+
+        def going(state):
+            return jnp.logical_and(state[0] > 0.02, state[1] < 24)
+
+        def squared(state):
+            for l in range(n_lam):
+                power = power_ref[l]
+                both = jnp.concatenate([power, inverse_ref[l].astype(BF16)], axis=1)
+                step = dot(power, both)
+                inverse_ref[l] = inverse_ref[l] + step[:, members:width]
+                power_ref[l] = step[:, 0:members].astype(BF16)
+            return state[0] * state[0], state[1] + 1
+
+        lax.while_loop(going, squared, (rate * rate, jnp.int32(0)))
+        inverses = [inverse_ref[l].astype(BF16) for l in range(n_lam)]
+        right_low = right.astype(BF16)
+        answers = [dot(inverse, right_low) for inverse in inverses]
+        high, low = halves(curvature)
+        wide = jnp.concatenate([high, low], axis=1)
+        sizes = []
+        for _ in range(2):
+            changes = []
+            for l in range(0, n_lam, 2):
+                pair = jnp.concatenate(answers[l : l + 2], axis=1)
+                top, bottom = halves(pair)
+                product = dot(wide, jnp.concatenate([top, top], axis=0)) + dot(high, bottom)
+                for q in range(2):
+                    part = product[:, q * members : (q + 1) * members]
+                    left = right - (part + shifts[l + q] * answers[l + q])
+                    changes.append(dot(inverses[l + q], left.astype(BF16)))
+            answers = [a + c for a, c in zip(answers, changes)]
+            sizes.append([jnp.max(jnp.abs(c), axis=0, keepdims=True) for c in changes])
+        good = None
+        for l in range(n_lam):
+            whole = jnp.max(jnp.max(jnp.abs(answers[l]), axis=0, keepdims=True))
+            first, second = jnp.max(sizes[0][l]), jnp.max(sizes[1][l])
+            fine = jnp.logical_and(second <= 1e-3 * whole, second <= jnp.maximum(0.2 * first, 1e-5 * whole))
+            good = fine if good is None else jnp.logical_and(good, fine)
+            answer_ref[l] = answers[l]
+
+        @pl.when(jnp.logical_not(good))
+        def _():
+            answer_ref[...] = jnp.zeros_like(answer_ref)
+
+            def improve(i, carry):
+                eliminate(lam_ref, full_ref, work_ref, answer_ref)
+                return carry
+
+            lax.fori_loop(0, 2, improve, 0)
+
+        transform = answer_ref[0].astype(BF16).astype(F32)
+        step = (iota((members, members), 0) - iota((members, members), 1)) % members
+        for start in (1, 1 + SPREAD):
+            excess = jnp.sum(transform, axis=0, keepdims=True) * (1.0 / SPREAD)
+            chosen = jnp.logical_and(step >= start, step < start + SPREAD)
+            moved = jnp.where(chosen, transform - excess, transform)
+            transform = moved.astype(BF16).astype(F32)
+        transform = transform.astype(BF16)
+        for i in range(count):
+            loads[i].wait()
+            x = hold_ref[i]
+            hold_ref[i] = (x.astype(F32) + dot(x, transform)).astype(BF16)
+            stores[i].start()
+        moments = gram_ref[...]
+        top, low = halves(moments)
+        rest = moments - top.astype(F32)
+        middle, low = halves(rest)
+        wide = jnp.concatenate([top, middle], axis=1)
+        for l in range(0, n_lam, 2):
+            pair = jnp.concatenate([answer_ref[l], answer_ref[l + 1]], axis=1).astype(BF16)
+            spread = dot(wide, jnp.concatenate([pair, pair], axis=0)) + dot(low, pair)
+            totals = jnp.sum(pair.astype(F32) * spread, axis=0, keepdims=True)
+            for q in range(2):
+                norm_ref[l + q : l + q + 1, :] = totals[:, q * members : (q + 1) * members]
+        for store in stores:
+            store.wait()
 
     return pl.pallas_call(
         body,
         out_shape=[
-            jax.ShapeDtypeStruct((width, members), BF16),
+            jax.ShapeDtypeStruct((cells, members), BF16),
             jax.ShapeDtypeStruct((n_lam, members), F32),
         ],
-        in_specs=[SMEM, SMEM] + [VMEM] * (n_obs + 1),
-        out_specs=[VMEM, VMEM],
+        in_specs=[SMEM, SMEM] + [VMEM] * (n_obs + 1) + [ANY],
+        out_specs=[ANY, VMEM],
         scratch_shapes=[
             pltpu.VMEM((members, width), F32),
             pltpu.VMEM((n_lam, members, width), F32),
+            pltpu.VMEM((n_lam, members, members), BF16),
+            pltpu.VMEM((n_lam, members, members), F32),
+            pltpu.VMEM((n_lam, members, members), F32),
+            pltpu.VMEM((count, chunk, members), BF16),
+            pltpu.SemaphoreType.DMA((count,)),
+            pltpu.SemaphoreType.DMA((count,)),
         ],
-        compiler_params=params(16),
-        cost_estimate=cost(1e9, 1e6),
-        name="solve_all",
-    )(place_obs, lambdas, *bands, field_gram)
-
-
-def field_moments(log_k, start, count, chunk):
+        compiler_params=params(52),
+        cost_estimate=cost(2e9, 4 * cells * members),
+        name="finish",
+    )(place_obs, lambdas, *bands, field_gram, log_k)
+
+
+def field_moments(log_k, total, first, chunk, count):
     members = log_k.shape[1]
-    first = start // chunk
-
-    def body(x_ref, out_ref):
-        x = x_ref[...]
+
+    def body(x_ref, total_ref, out_ref, hold_ref, sem):
+        copies = []
+        for i in range(count):
+            rows = pl.ds(first + i * chunk, chunk)
+            copies.append(pltpu.make_async_copy(x_ref.at[rows], hold_ref.at[i], sem.at[i]))
+            copies[i].start()
         spread = jnp.full((members, members), 1.0 / members, BF16)
-        anomalies = (x.astype(F32) - dot(x, spread)).astype(BF16)
-        part = dot(anomalies, anomalies, ((0,), (0,)))
-
-        @pl.when(pl.program_id(0) == 0)
-        def _():
-            out_ref[...] = part
-
-        @pl.when(pl.program_id(0) > 0)
-        def _():
-            out_ref[...] += part
-
-    return pl.pallas_call(
-        body,
-        grid=(count // chunk,),
+        moments = total_ref[...]
+        for i in range(count):
+            copies[i].wait()
+            x = hold_ref[i]
+            anomalies = (x.astype(F32) - dot(x, spread)).astype(BF16)
+            moments = moments + dot(anomalies, anomalies, ((0,), (0,)))
+        out_ref[...] = moments
+
+    return pl.pallas_call(
+        body,
         out_shape=jax.ShapeDtypeStruct((members, members), F32),
-        in_specs=[pl.BlockSpec((chunk, members), lambda i: (i + first, 0))],
-        out_specs=pl.BlockSpec((members, members), lambda i: (0, 0)),
-        compiler_params=params(16),
-        cost_estimate=cost(6.0e9, count * members * 2),
+        in_specs=[ANY, VMEM],
+        out_specs=VMEM,
+        scratch_shapes=[
+            pltpu.VMEM((count, chunk, members), BF16),
+            pltpu.SemaphoreType.DMA((count,)),
+        ],
+        compiler_params=params(52),
+        cost_estimate=cost(6.0e9, count * chunk * members * 2),
         name="field_moments",
-    )(log_k)
-
-
-def update_field(log_k, transform, chunk):
-    cells, members = log_k.shape
-
-    def body(x_ref, t_ref, out_ref):
-        x = x_ref[...]
-        change = dot(jnp.concatenate([x, x], axis=1), t_ref[...])
-        out_ref[...] = (x.astype(F32) + change).astype(BF16)
-
-    return pl.pallas_call(
-        body,
-        grid=(cells // chunk,),
-        out_shape=jax.ShapeDtypeStruct((cells, members), BF16),
-        in_specs=[
-            pl.BlockSpec((chunk, members), lambda i: (i, 0)),
-            pl.BlockSpec((2 * members, members), lambda i: (0, 0)),
-        ],
-        out_specs=pl.BlockSpec((chunk, members), lambda i: (i, 0)),
-        compiler_params=params(32),
-        cost_estimate=cost(4 * cells * members * members, 4 * cells * members),
-        name="update_field",
-    )(log_k, transform)
+    )(log_k, total)
+
+
+def sum_band(gathered, after):
+    n_tiles, band, width = gathered.shape
+
+    def body(gathered_ref, after_ref, out_ref):
+        total = gathered_ref[0].astype(F32)
+        for t in range(1, n_tiles):
+            total = total + gathered_ref[t].astype(F32)
+        out_ref[...] = total
+
+    return pl.pallas_call(
+        body,
+        out_shape=jax.ShapeDtypeStruct((band, width), F32),
+        in_specs=[VMEM, VMEM],
+        out_specs=VMEM,
+        compiler_params=params(8),
+        cost_estimate=cost(1e7, 1e6),
+        name="sum_band",
+    )(gathered, after)
 
 
 def shifted(array, axis, step):
@@ -309,31 +431,32 @@
 ):
     n_obs = lax.axis_size("obs")
     n_cell = lax.axis_size("cell")
-    wells_dev, members = obs_values.shape
+    members = heads_pred.shape[1]
     place_obs = lax.axis_index("obs").astype(jnp.int32).reshape(1)
-    sent = send_rows(slot_well, tile_count, heads_pred, n_obs, n_cell, wells_dev)
+    sent, own_wells = send_rows(
+        slot_well, tile_count, heads_pred, obs_values, obs_std, n_obs, n_cell
+    )
     received = lax.all_to_all(sent, "cell", split_axis=0, concat_axis=0, tiled=True)
-    own_wells = jnp.concatenate(
-        [obs_values, jnp.broadcast_to(obs_std[None], (EXTRA, wells_dev))], axis=0
-    )
     wells = [own_wells] + [shifted(own_wells, "obs", k) for k in range(1, n_obs)]
     cells = log_k.shape[0]
-    gram_a = field_moments(log_k, 0, cells // 2, 2048)
-    gram_b = field_moments(log_k, cells // 2, cells // 2, 2048)
+    chunk = cells // 6
+    moments = jnp.zeros((members, members), F32)
+    moments = field_moments(log_k, moments, 0, chunk, 3)
     column_blocks = jnp.arange(n_obs, dtype=jnp.int32) * n_cell + lax.axis_index("cell")
     weights = jnp.sum(
         taper[:, :, None]
         * (loc_blocks[:, :, None] == column_blocks[None, None, :]).astype(F32),
         axis=1,
     )
-    grams = block_grams(place_obs, received, wells, n_obs)
+    grams = block_grams(place_obs, received, wells, moments, n_obs)
     parts = [grams[0]] + [shifted(grams[k], "obs", k) for k in range(1, n_obs)]
     terms = tile_terms(weights, parts)
     gathered = lax.all_to_all(terms, "cell", split_axis=0, concat_axis=0, tiled=True)
-    own_band = jnp.sum(gathered.astype(F32), axis=0)
+    moments = field_moments(log_k, moments, 3 * chunk, chunk, 3)
+    own_band = sum_band(gathered, moments)
     bands = [own_band] + [shifted(own_band, "obs", k) for k in range(1, n_obs)]
-    transform, norms = solve_all(place_obs, lambdas, bands, gram_a + gram_b)
-    return (update_field(log_k, transform, 4096), norms[None])
+    posterior, norms = finish(place_obs, lambdas, bands, moments, log_k, 6)
+    return (posterior, norms[None])
 
 
 def solution(mesh):

time: 99.9 us -> 110 us (1.10); the launches traced: 98.2 us -> 110 us
  Pallas kernels: 48.1 us -> 63.2 us
  waiting for transfers between devices: 8.23 us -> 19.9 us
  local copies, waits for them, and re-layouts: 11.5 us -> 0.12 us
  starting transfers between devices: 27.3 us -> 25.1 us
  other arithmetic: 1.73 us -> 0.09 us
    pallas_call x5, Pallas kernels: 44.6 us -> 59.7 us  [the longest x1 45.1 us: finish(): pl.pallas_call(body, out_shape=[jax.ShapeDtypeStruct((cells, members), BF...]
    unnamed x12 -> x8, local copies, waits for them, and re-layouts: 10.7 us -> 0.02 us
    all_to_all x1, waiting for transfers between devices: 0.72 us -> 6.34 us  [on_device(): lax.all_to_all(sent, 'cell', split_axis=0, concat_axis=0, tiled=True)]
    all_to_all x1, waiting for transfers between devices: 0.01 us -> 5.53 us  [on_device(): lax.all_to_all(terms, 'cell', split_axis=0, concat_axis=0, tiled=True)]
    ppermute x9, starting transfers between devices: 14.2 us -> 12.9 us  [shifted(): return lax.ppermute(array, axis, [(i, (i + step) % n) for i in range(n)])]
  transfers between devices with their start and end apart: 11 -> 11, of which waited for: 6 -> 8; matrix products, arithmetic and copies ran while one was open for 2% -> 0% of each run, Pallas kernels for 15% -> 11%
where the time goes in v2:
time: 110 us
  Pallas kernels  63.2 us (57%)
  starting transfers between devices  25.1 us (23%)
  waiting for transfers between devices  19.9 us (18%)
  between operations  1.58 us (1%)
    pallas_call x1, Pallas kernels, finish(): pl.pallas_call(body, out_shape=[jax.ShapeDtypeStruct((cells, members), BF...  45.1 us
    ppermute x9, starting transfers between devices, shifted(): return lax.ppermute(array, axis, [(i, (i + step) % n) for i in range(n)])  12.9 us
    pallas_call x2, Pallas kernels, field_moments(): pl.pallas_call(body, out_shape=jax.ShapeDtypeStruct((members, members), F...  11.8 us
    all_to_all x1, starting transfers between devices, on_device(): lax.all_to_all(sent, 'cell', split_axis=0, concat_axis=0, tiled=True)  8.16 us
    ppermute x9, waiting for transfers between devices, shifted(): return lax.ppermute(array, axis, [(i, (i + step) % n) for i in range(n)])  8 us
    all_to_all x1, waiting for transfers between devices, on_device(): lax.all_to_all(sent, 'cell', split_axis=0, concat_axis=0, tiled=True)  6.34 us
    all_to_all x1, waiting for transfers between devices, on_device(): lax.all_to_all(terms, 'cell', split_axis=0, concat_axis=0, tiled=True)  5.53 us
    all_to_all x1, starting transfers between devices, on_device(): lax.all_to_all(terms, 'cell', split_axis=0, concat_axis=0, tiled=True)  4.07 us
  transfers between devices with their start and end apart: 11, of which 8 were waited for; matrix products, arithmetic and copies ran while one was open for 0% of the time, Pallas kernels for 11%

profile of v2, /device:TPU:0, one launch (start us, length us, event | category | flops | bytes accessed | tf_op | source)
XLA Modules:
  0.0 110.0 jit_solution(7104690205310190545)
XLA Ops:
  1.3 2.7 %send_rows.1 = (bf16[32,72,128]{2,1,0:T(8,128)(2,1)}, f32[136,128]{1,0:T(8,128)}) custom-call(s32[1]{0:T(128)S(6)} %copy.14.count_ref, s32[1,512]{1,0:T(1,128)} %bitcast.4, bf16[512,128]{1,0:T(8,128)(2,1)} %heads_ref.1, f32[128,128]{1,0:T(8,128)} %value_ref.1, f32[1,128]{1,0:T(1,128)} %bitcast.6), custom_call_target="tpu_custom_call" | custom-call | flops 1000000000 | bytes 1000000 | tf_op jit(solution)/shard_map/send_rows/pallas_call | solution.py:72
  4.0 0.0 copy-start.1
  4.0 3.1 %collective-permute-start.2 = (f32[136,128]{1,0:T(8,128)}, f32[136,128]{1,0:T(8,128)S(1)}, u32[]{:S(2)}, u32[]{:S(2)}) collective-permute-start(f32[136,128]{1,0:T(8,128)} %get-tuple-element.11.refs_0_), channel_id=1, source_target_pairs={{0,96},{32,0},{64,32},{96,64},{1,97},{33,1},{65,33},{97,65},{2,98}... | collective-permute-start | bytes 208904 | tf_op jit(solution)/shard_map/ppermute | solution.py:426
  7.1 0.6 collective-permute-start.1
  7.7 1.0 collective-permute-start
  8.7 8.2 %all-to-all-start = ((bf16[32,72,128]{2,1,0:T(8,128)(2,1)}), bf16[32,72,128]{2,1,0:T(8,128)(2,1)S(1)}, u32[]{:S(2)}, u32[]{:S(2)}) async-start(bf16[32,72,128]{2,1,0:T(8,128)(2,1)} %get-tuple-element.10), calls=%async_computation | async-start | bytes 1179648 | tf_op jit(solution)/shard_map/all_to_all | solution.py:439
  16.9 0.0 copy-start.2
  16.9 0.0 copy-start.3
  16.9 5.9 %field_moments.2.after_ref.total_ref = f32[128,128]{1,0:T(8,128)S(1)} custom-call(bf16[49152,128]{1,0:T(8,128)(2,1)} %refs_5_.1, f32[128,128]{1,0:T(8,128)S(1)} %broadcast_in_dim.4.total_ref), custom_call_target="tpu_custom_call" | custom-call | flops 6000000000 | bytes 6291456 | tf_op jit(solution)/shard_map/field_moments/pallas_call | solution.py:389
  22.8 0.0 collective-permute-done.2.refs_3_
  22.8 0.0 collective-permute-done.1.refs_2_
  22.8 0.0 collective-permute-done.refs_1_
  22.9 6.3 %all-to-all-done.recv_ref = bf16[32,72,128]{2,1,0:T(8,128)(2,1)S(1)} async-done(((bf16[32,72,128]{2,1,0:T(8,128)(2,1)}), bf16[32,72,128]{2,1,0:T(8,128)(2,1)S(1)}, u32[]{:S(2)}, u32[]{:S(2)}) %all-to-all-start) | async-done | bytes 589856 | tf_op jit(solution)/shard_map/all_to_all | solution.py:439
  29.2 0.0 copy-done.1
  29.2 1.6 %block_grams.1 = (bf16[4,32,256]{2,1,0:T(8,128)(2,1)S(1)}, bf16[4,32,256]{2,1,0:T(8,128)(2,1)S(1)}, bf16[4,32,256]{2,1,0:T(8,128)(2,1)S(1)}, bf16[4,32,256]{2,1,0:T(8,128)(2,1)S(1)}) custom-call(s32[1]{0:T(128)} %bitcast.me_ref, bf16[32,72,128]{2,1,0:T(8,128)(2,1)S(1)} %all-to-all-done.recv_ref, f32[128,128]{1,0:T(8,128)S(1)} %field_moments.2.after_ref.total_ref, ...), custom_call_target="tpu_custom_call" | custom-call | flops 1000000000 | bytes 1000000 | tf_op jit(solution)/shard_map/block_grams/pallas_call | solution.py:124
  30.8 0.0 copy-start
  30.9 2.0 %collective-permute-start.3 = (bf16[4,32,256]{2,1,0:T(8,128)(2,1)S(1)}, bf16[4,32,256]{2,1,0:T(8,128)(2,1)S(1)}, u32[]{:S(2)}, u32[]{:S(2)}) collective-permute-start(bf16[4,32,256]{2,1,0:T(8,128)(2,1)S(1)} %get-tuple-element.13), channel_id=1, source_target_pairs={{0,32},{32,64},{64,96},{96,0},{1,33},{33,65},{65,97},{97,1},{2,34}... | collective-permute-start | bytes 196616 | tf_op jit(solution)/shard_map/ppermute | solution.py:426
  32.8 1.8 %collective-permute-start.4 = (bf16[4,32,256]{2,1,0:T(8,128)(2,1)S(1)}, bf16[4,32,256]{2,1,0:T(8,128)(2,1)S(1)}, u32[]{:S(2)}, u32[]{:S(2)}) collective-permute-start(bf16[4,32,256]{2,1,0:T(8,128)(2,1)S(1)} %get-tuple-element.14), channel_id=1, source_target_pairs={{0,64},{32,96},{64,0},{96,32},{1,65},{33,97},{65,1},{97,33},{2,66}... | collective-permute-start | bytes 196616 | tf_op jit(solution)/shard_map/ppermute | solution.py:426
  34.6 0.9 collective-permute-start.5
  35.6 0.0 copy-done.2
  35.6 0.0 copy-done.3
  35.6 0.1 select_reduce_fusion
  35.7 0.1 copy.13.weight_ref
  35.8 0.6 collective-permute-done.3.refs_1_
  36.4 2.2 %collective-permute-done.4.refs_2_ = bf16[4,32,256]{2,1,0:T(8,128)(2,1)S(1)} collective-permute-done((bf16[4,32,256]{2,1,0:T(8,128)(2,1)S(1)}, bf16[4,32,256]{2,1,0:T(8,128)(2,1)S(1)}, u32[]{:S(2)}, u32[]{:S(2)}) %collective-permute-start.4) | collective-permute-done | bytes 65568 | tf_op jit(solution)/shard_map/ppermute | solution.py:426
  38.6 0.3 collective-permute-done.5.refs_3_
  38.9 1.9 %tile_terms.1 = bf16[32,32,256]{2,1,0:T(8,128)(2,1)} custom-call(f32[32,4]{1,0:T(8,128)S(1)} %copy.13.weight_ref, bf16[4,32,256]{2,1,0:T(8,128)(2,1)S(1)} %get-tuple-element.12.refs_0_, bf16[4,32,256]{2,1,0:T(8,128)(2,1)S(1)} %collective-permute-done.3.refs_1_, bf16[4,32,256]{2,1,0:T(8,128)(2,1)S(1)} %collective-permute-done.4.refs_2_, ...), custom_call_target="tpu_custom_call" | custom-call | flops 100000000 | bytes 1000000 | tf_op jit(solution)/shard_map/tile_terms/pallas_call | solution.py:154
  40.8 4.1 %all-to-all-start.1 = ((bf16[32,32,256]{2,1,0:T(8,128)(2,1)}), bf16[32,32,256]{2,1,0:T(8,128)(2,1)S(1)}, u32[]{:S(2)}, u32[]{:S(2)}) async-start(bf16[32,32,256]{2,1,0:T(8,128)(2,1)} %tile_terms.1), calls=%async_computation.1 | async-start | bytes 1048576 | tf_op jit(solution)/shard_map/all_to_all | solution.py:454
  44.9 5.9 %field_moments.3.after_ref.refs_4_ = f32[128,128]{1,0:T(8,128)S(1)} custom-call(bf16[49152,128]{1,0:T(8,128)(2,1)} %refs_5_.1, f32[128,128]{1,0:T(8,128)S(1)} %field_moments.2.after_ref.total_ref), custom_call_target="tpu_custom_call" | custom-call | flops 6000000000 | bytes 6291456 | tf_op jit(solution)/shard_map/field_moments/pallas_call | solution.py:389
  50.8 5.5 %all-to-all-done.1.gathered_ref = bf16[32,32,256]{2,1,0:T(8,128)(2,1)S(1)} async-done(((bf16[32,32,256]{2,1,0:T(8,128)(2,1)}), bf16[32,32,256]{2,1,0:T(8,128)(2,1)S(1)}, u32[]{:S(2)}, u32[]{:S(2)}) %all-to-all-start.1) | async-done | bytes 524320 | tf_op jit(solution)/shard_map/all_to_all | solution.py:454
  56.3 0.1 sum_band.1.refs_0_
  56.4 2.5 %collective-permute-start.8 = (f32[32,256]{1,0:T(8,128)S(1)}, f32[32,256]{1,0:T(8,128)S(1)}, u32[]{:S(2)}, u32[]{:S(2)}) collective-permute-start(f32[32,256]{1,0:T(8,128)S(1)} %sum_band.1.refs_0_), channel_id=1, source_target_pairs={{0,96},{32,0},{64,32},{96,64},{1,97},{33,1},{65,33},{97,65},{2,98}... | collective-permute-start | bytes 98312 | tf_op jit(solution)/shard_map/ppermute | solution.py:426
  58.8 0.7 collective-permute-start.7
  59.5 0.3 collective-permute-start.6
  59.8 0.6 collective-permute-done.8.refs_3_
  60.4 3.8 %collective-permute-done.7.refs_2_ = f32[32,256]{1,0:T(8,128)S(1)} collective-permute-done((f32[32,256]{1,0:T(8,128)S(1)}, f32[32,256]{1,0:T(8,128)S(1)}, u32[]{:S(2)}, u32[]{:S(2)}) %collective-permute-start.7) | collective-permute-done | bytes 32800 | tf_op jit(solution)/shard_map/ppermute | solution.py:426
  64.3 0.4 collective-permute-done.6.refs_1_
  64.6 0.0 copy-done
  64.6 45.1 %finish.1 = (bf16[49152,128]{1,0:T(8,128)(2,1)}, f32[4,128]{1,0:T(4,128)}) custom-call(s32[1]{0:T(128)} %bitcast.me_ref, f32[4]{0:T(128)S(1)} %copy-done, f32[32,256]{1,0:T(8,128)S(1)} %sum_band.1.refs_0_, f32[32,256]{1,0:T(8,128)S(1)} %collective-permute-done.6.refs_1_, f32[32,256]{1,0:T(8,128)S(1)} %collective-permute-done.7.refs_2_, ...), custom_call_target="tpu_custom_call" | custom-call | flops 2000000000 | bytes 25165824 | tf_op jit(solution)/shard_map/finish/pallas_call | solution.py:347
  (2 shorter events, 0.0 us)
Async XLA Ops:
  4.0 25.2 %copy-start.1 = (f32[136,128]{1,0:T(8,128)S(1)}, f32[136,128]{1,0:T(8,128)}, u32[]{:S(2)}) copy-start(f32[136,128]{1,0:T(8,128)} %get-tuple-element.11.refs_0_) | copy-start | bytes 208900
  4.0 18.8 %collective-permute-start.2 = (f32[136,128]{1,0:T(8,128)}, f32[136,128]{1,0:T(8,128)S(1)}, u32[]{:S(2)}, u32[]{:S(2)}) collective-permute-start(f32[136,128]{1,0:T(8,128)} %get-tuple-element.11.refs_0_), channel_id=1, source_target_pairs={{0,96},{32,0},{64,32},{96,64},{1,97},{33,1},{65,33},{97,65},{2,98}... | collective-permute-start | bytes 208904 | tf_op jit(solution)/shard_map/ppermute | solution.py:426
  7.1 15.7 %collective-permute-start.1 = (f32[136,128]{1,0:T(8,128)}, f32[136,128]{1,0:T(8,128)S(1)}, u32[]{:S(2)}, u32[]{:S(2)}) collective-permute-start(f32[136,128]{1,0:T(8,128)} %get-tuple-element.11.refs_0_), channel_id=1, source_target_pairs={{0,64},{32,96},{64,0},{96,32},{1,65},{33,97},{65,1},{97,33},{2,66}... | collective-permute-start | bytes 208904 | tf_op jit(solution)/shard_map/ppermute | solution.py:426
  7.7 15.1 %collective-permute-start = (f32[136,128]{1,0:T(8,128)}, f32[136,128]{1,0:T(8,128)S(1)}, u32[]{:S(2)}, u32[]{:S(2)}) collective-permute-start(f32[136,128]{1,0:T(8,128)} %get-tuple-element.11.refs_0_), channel_id=1, source_target_pairs={{0,32},{32,64},{64,96},{96,0},{1,33},{33,65},{65,97},{97,1},{2,34}... | collective-permute-start | bytes 208904 | tf_op jit(solution)/shard_map/ppermute | solution.py:426
  8.7 20.5 %all-to-all-start = ((bf16[32,72,128]{2,1,0:T(8,128)(2,1)}), bf16[32,72,128]{2,1,0:T(8,128)(2,1)S(1)}, u32[]{:S(2)}, u32[]{:S(2)}) async-start(bf16[32,72,128]{2,1,0:T(8,128)(2,1)} %get-tuple-element.10), calls=%async_computation | async-start | bytes 1179648 | tf_op jit(solution)/shard_map/all_to_all | solution.py:439
  16.9 18.7 %copy-start.2 = (f32[32,8]{0,1:T(8,128)S(1)}, f32[32,8]{0,1:T(8,128)}, u32[]{:S(2)}) copy-start(f32[32,8]{0,1:T(8,128)} %param.16) | copy-start | bytes 3076
  16.9 18.7 %copy-start.3 = (s32[32,8]{0,1:T(8,128)S(1)}, s32[32,8]{0,1:T(8,128)}, u32[]{:S(2)}) copy-start(s32[32,8]{0,1:T(8,128)} %param.15) | copy-start | bytes 3076
  30.8 33.8 %copy-start = (f32[4]{0:T(128)S(1)}, f32[4]{0:T(128)}, u32[]{:S(2)}) copy-start(f32[4]{0:T(128)} %lam_ref.1) | copy-start | bytes 52
  30.9 5.5 %collective-permute-start.3 = (bf16[4,32,256]{2,1,0:T(8,128)(2,1)S(1)}, bf16[4,32,256]{2,1,0:T(8,128)(2,1)S(1)}, u32[]{:S(2)}, u32[]{:S(2)}) collective-permute-start(bf16[4,32,256]{2,1,0:T(8,128)(2,1)S(1)} %get-tuple-element.13), channel_id=1, source_target_pairs={{0,32},{32,64},{64,96},{96,0},{1,33},{33,65},{65,97},{97,1},{2,34}... | collective-permute-start | bytes 196616 | tf_op jit(solution)/shard_map/ppermute | solution.py:426
  32.8 5.8 %collective-permute-start.4 = (bf16[4,32,256]{2,1,0:T(8,128)(2,1)S(1)}, bf16[4,32,256]{2,1,0:T(8,128)(2,1)S(1)}, u32[]{:S(2)}, u32[]{:S(2)}) collective-permute-start(bf16[4,32,256]{2,1,0:T(8,128)(2,1)S(1)} %get-tuple-element.14), channel_id=1, source_target_pairs={{0,64},{32,96},{64,0},{96,32},{1,65},{33,97},{65,1},{97,33},{2,66}... | collective-permute-start | bytes 196616 | tf_op jit(solution)/shard_map/ppermute | solution.py:426
  34.6 4.3 %collective-permute-start.5 = (bf16[4,32,256]{2,1,0:T(8,128)(2,1)S(1)}, bf16[4,32,256]{2,1,0:T(8,128)(2,1)S(1)}, u32[]{:S(2)}, u32[]{:S(2)}) collective-permute-start(bf16[4,32,256]{2,1,0:T(8,128)(2,1)S(1)} %get-tuple-element.15), channel_id=1, source_target_pairs={{0,96},{32,0},{64,32},{96,64},{1,97},{33,1},{65,33},{97,65},{2,98}... | collective-permute-start | bytes 196616 | tf_op jit(solution)/shard_map/ppermute | solution.py:426
  40.8 15.5 %all-to-all-start.1 = ((bf16[32,32,256]{2,1,0:T(8,128)(2,1)}), bf16[32,32,256]{2,1,0:T(8,128)(2,1)S(1)}, u32[]{:S(2)}, u32[]{:S(2)}) async-start(bf16[32,32,256]{2,1,0:T(8,128)(2,1)} %tile_terms.1), calls=%async_computation.1 | async-start | bytes 1048576 | tf_op jit(solution)/shard_map/all_to_all | solution.py:454
  56.4 4.1 %collective-permute-start.8 = (f32[32,256]{1,0:T(8,128)S(1)}, f32[32,256]{1,0:T(8,128)S(1)}, u32[]{:S(2)}, u32[]{:S(2)}) collective-permute-start(f32[32,256]{1,0:T(8,128)S(1)} %sum_band.1.refs_0_), channel_id=1, source_target_pairs={{0,96},{32,0},{64,32},{96,64},{1,97},{33,1},{65,33},{97,65},{2,98}... | collective-permute-start | bytes 98312 | tf_op jit(solution)/shard_map/ppermute | solution.py:426
  58.8 5.4 %collective-permute-start.7 = (f32[32,256]{1,0:T(8,128)S(1)}, f32[32,256]{1,0:T(8,128)S(1)}, u32[]{:S(2)}, u32[]{:S(2)}) collective-permute-start(f32[32,256]{1,0:T(8,128)S(1)} %sum_band.1.refs_0_), channel_id=1, source_target_pairs={{0,64},{32,96},{64,0},{96,32},{1,65},{33,97},{65,1},{97,33},{2,66}... | collective-permute-start | bytes 98312 | tf_op jit(solution)/shard_map/ppermute | solution.py:426
  59.5 5.1 %collective-permute-start.6 = (f32[32,256]{1,0:T(8,128)S(1)}, f32[32,256]{1,0:T(8,128)S(1)}, u32[]{:S(2)}, u32[]{:S(2)}) collective-permute-start(f32[32,256]{1,0:T(8,128)S(1)} %sum_band.1.refs_0_), channel_id=1, source_target_pairs={{0,32},{32,64},{64,96},{96,0},{1,33},{33,65},{65,97},{97,1},{2,34}... | collective-permute-start | bytes 98312 | tf_op jit(solution)/shard_map/ppermute | solution.py:426

commit v3 on v2

--- a/solution.py
+++ b/solution.py
@@ -9,6 +9,7 @@
 CAP = 16
 EXTRA = 8
 SPREAD = 16
+TILE = 512
 F32 = jnp.float32
 BF16 = jnp.bfloat16
 HIGHEST = lax.Precision.HIGHEST
@@ -235,12 +236,12 @@
         band_refs = refs[:n_obs]
         gram_ref, field_ref, out_ref, norm_ref = refs[n_obs : n_obs + 4]
         full_ref, work_ref, power_ref, inverse_ref, answer_ref = refs[n_obs + 4 : n_obs + 9]
-        hold_ref, in_sem, out_sem = refs[n_obs + 9 :]
+        hold_ref, made_ref, in_sem, out_sem = refs[n_obs + 9 :]
         loads, stores = [], []
         for i in range(count):
             rows = pl.ds(i * chunk, chunk)
             loads.append(pltpu.make_async_copy(field_ref.at[rows], hold_ref.at[i], in_sem.at[i]))
-            stores.append(pltpu.make_async_copy(hold_ref.at[i], out_ref.at[rows], out_sem.at[i]))
+            stores.append(pltpu.make_async_copy(made_ref.at[i], out_ref.at[rows], out_sem.at[i]))
             loads[i].start()
         me = me_ref[0]
         for k in range(n_obs):
@@ -327,8 +328,10 @@
         transform = transform.astype(BF16)
         for i in range(count):
             loads[i].wait()
-            x = hold_ref[i]
-            hold_ref[i] = (x.astype(F32) + dot(x, transform)).astype(BF16)
+            for at in range(0, chunk, TILE):
+                x = hold_ref[i, at : at + TILE, :]
+                updated = x.astype(F32) + dot(x, transform)
+                made_ref[i, at : at + TILE, :] = updated.astype(BF16)
             stores[i].start()
         moments = gram_ref[...]
         top, low = halves(moments)
@@ -359,6 +362,7 @@
             pltpu.VMEM((n_lam, members, members), F32),
             pltpu.VMEM((n_lam, members, members), F32),
             pltpu.VMEM((count, chunk, members), BF16),
+            pltpu.VMEM((count, chunk, members), BF16),
             pltpu.SemaphoreType.DMA((count,)),
             pltpu.SemaphoreType.DMA((count,)),
         ],
@@ -377,12 +381,12 @@
             rows = pl.ds(first + i * chunk, chunk)
             copies.append(pltpu.make_async_copy(x_ref.at[rows], hold_ref.at[i], sem.at[i]))
             copies[i].start()
-        spread = jnp.full((members, members), 1.0 / members, BF16)
+        eye = iota((members, members), 0) == iota((members, members), 1)
+        centre = (jnp.where(eye, 1.0, 0.0) - 1.0 / members).astype(BF16)
         moments = total_ref[...]
         for i in range(count):
             copies[i].wait()
-            x = hold_ref[i]
-            anomalies = (x.astype(F32) - dot(x, spread)).astype(BF16)
+            anomalies = dot(hold_ref[i], centre).astype(BF16)
             moments = moments + dot(anomalies, anomalies, ((0,), (0,)))
         out_ref[...] = moments
 
@@ -441,7 +445,7 @@
     cells = log_k.shape[0]
     chunk = cells // 6
     moments = jnp.zeros((members, members), F32)
-    moments = field_moments(log_k, moments, 0, chunk, 3)
+    moments = field_moments(log_k, moments, 0, chunk, 2)
     column_blocks = jnp.arange(n_obs, dtype=jnp.int32) * n_cell + lax.axis_index("cell")
     weights = jnp.sum(
         taper[:, :, None]
@@ -452,7 +456,7 @@
     parts = [grams[0]] + [shifted(grams[k], "obs", k) for k in range(1, n_obs)]
     terms = tile_terms(weights, parts)
     gathered = lax.all_to_all(terms, "cell", split_axis=0, concat_axis=0, tiled=True)
-    moments = field_moments(log_k, moments, 3 * chunk, chunk, 3)
+    moments = field_moments(log_k, moments, 2 * chunk, chunk, 4)
     own_band = sum_band(gathered, moments)
     bands = [own_band] + [shifted(own_band, "obs", k) for k in range(1, n_obs)]
     posterior, norms = finish(place_obs, lambdas, bands, moments, log_k, 6)

time: 110 us -> 107 us (0.973)
  Pallas kernels: 63.2 us -> 60 us
    pallas_call x1, Pallas kernels: 45.1 us -> 41.9 us  [finish(): pl.pallas_call(body, out_shape=[jax.ShapeDtypeStruct((cells, members), BF...]
    all_to_all x1, waiting for transfers between devices: 6.34 us -> 7.77 us  [on_device(): lax.all_to_all(sent, 'cell', split_axis=0, concat_axis=0, tiled=True)]
    all_to_all x1, waiting for transfers between devices: 5.53 us -> 4.11 us  [on_device(): lax.all_to_all(terms, 'cell', split_axis=0, concat_axis=0, tiled=True)]
where the time goes in v3:
time: 107 us
  Pallas kernels  60 us (56%)
  starting transfers between devices  25.1 us (23%)
  waiting for transfers between devices  19.9 us (19%)
  between operations  1.58 us (1%)
    pallas_call x1, Pallas kernels, finish(): pl.pallas_call(body, out_shape=[jax.ShapeDtypeStruct((cells, members), BF...  41.9 us
    ppermute x9, starting transfers between devices, shifted(): return lax.ppermute(array, axis, [(i, (i + step) % n) for i in range(n)])  12.9 us
    pallas_call x2, Pallas kernels, field_moments(): pl.pallas_call(body, out_shape=jax.ShapeDtypeStruct((members, members), F...  11.7 us
    all_to_all x1, starting transfers between devices, on_device(): lax.all_to_all(sent, 'cell', split_axis=0, concat_axis=0, tiled=True)  8.16 us
    ppermute x9, waiting for transfers between devices, shifted(): return lax.ppermute(array, axis, [(i, (i + step) % n) for i in range(n)])  8 us
    all_to_all x1, waiting for transfers between devices, on_device(): lax.all_to_all(sent, 'cell', split_axis=0, concat_axis=0, tiled=True)  7.77 us
    all_to_all x1, waiting for transfers between devices, on_device(): lax.all_to_all(terms, 'cell', split_axis=0, concat_axis=0, tiled=True)  4.11 us
    all_to_all x1, starting transfers between devices, on_device(): lax.all_to_all(terms, 'cell', split_axis=0, concat_axis=0, tiled=True)  4.07 us
  transfers between devices with their start and end apart: 11, of which 8 were waited for; matrix products, arithmetic and copies ran while one was open for 0% of the time, Pallas kernels for 11%

profile of v3, /device:TPU:0, one launch (start us, length us, event | category | flops | bytes accessed | tf_op | source)
XLA Modules:
  0.0 106.8 jit_solution(17207995565418417234)
XLA Ops:
  1.3 2.7 %send_rows.1 = (bf16[32,72,128]{2,1,0:T(8,128)(2,1)}, f32[136,128]{1,0:T(8,128)}) custom-call(s32[1]{0:T(128)S(6)} %copy.14.count_ref, s32[1,512]{1,0:T(1,128)} %bitcast.4, bf16[512,128]{1,0:T(8,128)(2,1)} %heads_ref.1, f32[128,128]{1,0:T(8,128)} %value_ref.1, f32[1,128]{1,0:T(1,128)} %bitcast.6), custom_call_target="tpu_custom_call" | custom-call | flops 1000000000 | bytes 1000000 | tf_op jit(solution)/shard_map/send_rows/pallas_call | solution.py:73
  4.0 0.0 copy-start.1
  4.0 3.1 %collective-permute-start.2 = (f32[136,128]{1,0:T(8,128)}, f32[136,128]{1,0:T(8,128)S(1)}, u32[]{:S(2)}, u32[]{:S(2)}) collective-permute-start(f32[136,128]{1,0:T(8,128)} %get-tuple-element.11.refs_0_), channel_id=1, source_target_pairs={{0,96},{32,0},{64,32},{96,64},{1,97},{33,1},{65,33},{97,65},{2,98}... | collective-permute-start | bytes 208904 | tf_op jit(solution)/shard_map/ppermute | solution.py:430
  7.1 0.6 collective-permute-start.1
  7.7 1.0 collective-permute-start
  8.7 8.2 %all-to-all-start = ((bf16[32,72,128]{2,1,0:T(8,128)(2,1)}), bf16[32,72,128]{2,1,0:T(8,128)(2,1)S(1)}, u32[]{:S(2)}, u32[]{:S(2)}) async-start(bf16[32,72,128]{2,1,0:T(8,128)(2,1)} %get-tuple-element.10), calls=%async_computation | async-start | bytes 1179648 | tf_op jit(solution)/shard_map/all_to_all | solution.py:443
  16.9 0.0 copy-start.2
  16.9 0.0 copy-start.3
  16.9 4.5 %field_moments.2.after_ref.total_ref = f32[128,128]{1,0:T(8,128)S(1)} custom-call(bf16[49152,128]{1,0:T(8,128)(2,1)} %refs_5_.1, f32[128,128]{1,0:T(8,128)S(1)} %broadcast_in_dim.4.total_ref), custom_call_target="tpu_custom_call" | custom-call | flops 6000000000 | bytes 4194304 | tf_op jit(solution)/shard_map/field_moments/pallas_call | solution.py:393
  21.4 0.0 collective-permute-done.2.refs_3_
  21.4 0.0 collective-permute-done.1.refs_2_
  21.4 0.0 collective-permute-done.refs_1_
  21.4 7.8 %all-to-all-done.recv_ref = bf16[32,72,128]{2,1,0:T(8,128)(2,1)S(1)} async-done(((bf16[32,72,128]{2,1,0:T(8,128)(2,1)}), bf16[32,72,128]{2,1,0:T(8,128)(2,1)S(1)}, u32[]{:S(2)}, u32[]{:S(2)}) %all-to-all-start) | async-done | bytes 589856 | tf_op jit(solution)/shard_map/all_to_all | solution.py:443
  29.2 0.0 copy-done.1
  29.2 1.6 %block_grams.1 = (bf16[4,32,256]{2,1,0:T(8,128)(2,1)S(1)}, bf16[4,32,256]{2,1,0:T(8,128)(2,1)S(1)}, bf16[4,32,256]{2,1,0:T(8,128)(2,1)S(1)}, bf16[4,32,256]{2,1,0:T(8,128)(2,1)S(1)}) custom-call(s32[1]{0:T(128)} %bitcast.me_ref, bf16[32,72,128]{2,1,0:T(8,128)(2,1)S(1)} %all-to-all-done.recv_ref, f32[128,128]{1,0:T(8,128)S(1)} %field_moments.2.after_ref.total_ref, ...), custom_call_target="tpu_custom_call" | custom-call | flops 1000000000 | bytes 1000000 | tf_op jit(solution)/shard_map/block_grams/pallas_call | solution.py:125
  30.8 0.0 copy-start
  30.9 2.0 %collective-permute-start.3 = (bf16[4,32,256]{2,1,0:T(8,128)(2,1)S(1)}, bf16[4,32,256]{2,1,0:T(8,128)(2,1)S(1)}, u32[]{:S(2)}, u32[]{:S(2)}) collective-permute-start(bf16[4,32,256]{2,1,0:T(8,128)(2,1)S(1)} %get-tuple-element.13), channel_id=1, source_target_pairs={{0,32},{32,64},{64,96},{96,0},{1,33},{33,65},{65,97},{97,1},{2,34}... | collective-permute-start | bytes 196616 | tf_op jit(solution)/shard_map/ppermute | solution.py:430
  32.8 1.8 %collective-permute-start.4 = (bf16[4,32,256]{2,1,0:T(8,128)(2,1)S(1)}, bf16[4,32,256]{2,1,0:T(8,128)(2,1)S(1)}, u32[]{:S(2)}, u32[]{:S(2)}) collective-permute-start(bf16[4,32,256]{2,1,0:T(8,128)(2,1)S(1)} %get-tuple-element.14), channel_id=1, source_target_pairs={{0,64},{32,96},{64,0},{96,32},{1,65},{33,97},{65,1},{97,33},{2,66}... | collective-permute-start | bytes 196616 | tf_op jit(solution)/shard_map/ppermute | solution.py:430
  34.6 0.9 collective-permute-start.5
  35.6 0.0 copy-done.2
  35.6 0.0 copy-done.3
  35.6 0.1 select_reduce_fusion
  35.7 0.1 copy.13.weight_ref
  35.8 0.6 collective-permute-done.3.refs_1_
  36.4 2.2 %collective-permute-done.4.refs_2_ = bf16[4,32,256]{2,1,0:T(8,128)(2,1)S(1)} collective-permute-done((bf16[4,32,256]{2,1,0:T(8,128)(2,1)S(1)}, bf16[4,32,256]{2,1,0:T(8,128)(2,1)S(1)}, u32[]{:S(2)}, u32[]{:S(2)}) %collective-permute-start.4) | collective-permute-done | bytes 65568 | tf_op jit(solution)/shard_map/ppermute | solution.py:430
  38.6 0.3 collective-permute-done.5.refs_3_
  38.9 1.9 %tile_terms.1 = bf16[32,32,256]{2,1,0:T(8,128)(2,1)} custom-call(f32[32,4]{1,0:T(8,128)S(1)} %copy.13.weight_ref, bf16[4,32,256]{2,1,0:T(8,128)(2,1)S(1)} %get-tuple-element.12.refs_0_, bf16[4,32,256]{2,1,0:T(8,128)(2,1)S(1)} %collective-permute-done.3.refs_1_, bf16[4,32,256]{2,1,0:T(8,128)(2,1)S(1)} %collective-permute-done.4.refs_2_, ...), custom_call_target="tpu_custom_call" | custom-call | flops 100000000 | bytes 1000000 | tf_op jit(solution)/shard_map/tile_terms/pallas_call | solution.py:155
  40.8 4.1 %all-to-all-start.1 = ((bf16[32,32,256]{2,1,0:T(8,128)(2,1)}), bf16[32,32,256]{2,1,0:T(8,128)(2,1)S(1)}, u32[]{:S(2)}, u32[]{:S(2)}) async-start(bf16[32,32,256]{2,1,0:T(8,128)(2,1)} %tile_terms.1), calls=%async_computation.1 | async-start | bytes 1048576 | tf_op jit(solution)/shard_map/all_to_all | solution.py:458
  44.9 7.3 %field_moments.3.after_ref.refs_4_ = f32[128,128]{1,0:T(8,128)S(1)} custom-call(bf16[49152,128]{1,0:T(8,128)(2,1)} %refs_5_.1, f32[128,128]{1,0:T(8,128)S(1)} %field_moments.2.after_ref.total_ref), custom_call_target="tpu_custom_call" | custom-call | flops 6000000000 | bytes 8388608 | tf_op jit(solution)/shard_map/field_moments/pallas_call | solution.py:393
  52.2 4.1 %all-to-all-done.1.gathered_ref = bf16[32,32,256]{2,1,0:T(8,128)(2,1)S(1)} async-done(((bf16[32,32,256]{2,1,0:T(8,128)(2,1)}), bf16[32,32,256]{2,1,0:T(8,128)(2,1)S(1)}, u32[]{:S(2)}, u32[]{:S(2)}) %all-to-all-start.1) | async-done | bytes 524320 | tf_op jit(solution)/shard_map/all_to_all | solution.py:458
  56.3 0.1 sum_band.1.refs_0_
  56.4 2.5 %collective-permute-start.8 = (f32[32,256]{1,0:T(8,128)S(1)}, f32[32,256]{1,0:T(8,128)S(1)}, u32[]{:S(2)}, u32[]{:S(2)}) collective-permute-start(f32[32,256]{1,0:T(8,128)S(1)} %sum_band.1.refs_0_), channel_id=1, source_target_pairs={{0,96},{32,0},{64,32},{96,64},{1,97},{33,1},{65,33},{97,65},{2,98}... | collective-permute-start | bytes 98312 | tf_op jit(solution)/shard_map/ppermute | solution.py:430
  58.8 0.7 collective-permute-start.7
  59.5 0.3 collective-permute-start.6
  59.8 0.6 collective-permute-done.8.refs_3_
  60.4 3.8 %collective-permute-done.7.refs_2_ = f32[32,256]{1,0:T(8,128)S(1)} collective-permute-done((f32[32,256]{1,0:T(8,128)S(1)}, f32[32,256]{1,0:T(8,128)S(1)}, u32[]{:S(2)}, u32[]{:S(2)}) %collective-permute-start.7) | collective-permute-done | bytes 32800 | tf_op jit(solution)/shard_map/ppermute | solution.py:430
  64.3 0.4 collective-permute-done.6.refs_1_
  64.6 0.0 copy-done
  64.6 41.9 %finish.1 = (bf16[49152,128]{1,0:T(8,128)(2,1)}, f32[4,128]{1,0:T(4,128)}) custom-call(s32[1]{0:T(128)} %bitcast.me_ref, f32[4]{0:T(128)S(1)} %copy-done, f32[32,256]{1,0:T(8,128)S(1)} %sum_band.1.refs_0_, f32[32,256]{1,0:T(8,128)S(1)} %collective-permute-done.6.refs_1_, f32[32,256]{1,0:T(8,128)S(1)} %collective-permute-done.7.refs_2_, ...), custom_call_target="tpu_custom_call" | custom-call | flops 2000000000 | bytes 25165824 | tf_op jit(solution)/shard_map/finish/pallas_call | solution.py:350
  (2 shorter events, 0.0 us)
Async XLA Ops:
  4.0 25.2 %copy-start.1 = (f32[136,128]{1,0:T(8,128)S(1)}, f32[136,128]{1,0:T(8,128)}, u32[]{:S(2)}) copy-start(f32[136,128]{1,0:T(8,128)} %get-tuple-element.11.refs_0_) | copy-start | bytes 208900
  4.0 17.4 %collective-permute-start.2 = (f32[136,128]{1,0:T(8,128)}, f32[136,128]{1,0:T(8,128)S(1)}, u32[]{:S(2)}, u32[]{:S(2)}) collective-permute-start(f32[136,128]{1,0:T(8,128)} %get-tuple-element.11.refs_0_), channel_id=1, source_target_pairs={{0,96},{32,0},{64,32},{96,64},{1,97},{33,1},{65,33},{97,65},{2,98}... | collective-permute-start | bytes 208904 | tf_op jit(solution)/shard_map/ppermute | solution.py:430
  7.1 14.3 %collective-permute-start.1 = (f32[136,128]{1,0:T(8,128)}, f32[136,128]{1,0:T(8,128)S(1)}, u32[]{:S(2)}, u32[]{:S(2)}) collective-permute-start(f32[136,128]{1,0:T(8,128)} %get-tuple-element.11.refs_0_), channel_id=1, source_target_pairs={{0,64},{32,96},{64,0},{96,32},{1,65},{33,97},{65,1},{97,33},{2,66}... | collective-permute-start | bytes 208904 | tf_op jit(solution)/shard_map/ppermute | solution.py:430
  7.7 13.7 %collective-permute-start = (f32[136,128]{1,0:T(8,128)}, f32[136,128]{1,0:T(8,128)S(1)}, u32[]{:S(2)}, u32[]{:S(2)}) collective-permute-start(f32[136,128]{1,0:T(8,128)} %get-tuple-element.11.refs_0_), channel_id=1, source_target_pairs={{0,32},{32,64},{64,96},{96,0},{1,33},{33,65},{65,97},{97,1},{2,34}... | collective-permute-start | bytes 208904 | tf_op jit(solution)/shard_map/ppermute | solution.py:430
  8.7 20.5 %all-to-all-start = ((bf16[32,72,128]{2,1,0:T(8,128)(2,1)}), bf16[32,72,128]{2,1,0:T(8,128)(2,1)S(1)}, u32[]{:S(2)}, u32[]{:S(2)}) async-start(bf16[32,72,128]{2,1,0:T(8,128)(2,1)} %get-tuple-element.10), calls=%async_computation | async-start | bytes 1179648 | tf_op jit(solution)/shard_map/all_to_all | solution.py:443
  16.9 18.7 %copy-start.2 = (f32[32,8]{0,1:T(8,128)S(1)}, f32[32,8]{0,1:T(8,128)}, u32[]{:S(2)}) copy-start(f32[32,8]{0,1:T(8,128)} %param.16) | copy-start | bytes 3076
  16.9 18.7 %copy-start.3 = (s32[32,8]{0,1:T(8,128)S(1)}, s32[32,8]{0,1:T(8,128)}, u32[]{:S(2)}) copy-start(s32[32,8]{0,1:T(8,128)} %param.15) | copy-start | bytes 3076
  30.8 33.8 %copy-start = (f32[4]{0:T(128)S(1)}, f32[4]{0:T(128)}, u32[]{:S(2)}) copy-start(f32[4]{0:T(128)} %lam_ref.1) | copy-start | bytes 52
  30.9 5.5 %collective-permute-start.3 = (bf16[4,32,256]{2,1,0:T(8,128)(2,1)S(1)}, bf16[4,32,256]{2,1,0:T(8,128)(2,1)S(1)}, u32[]{:S(2)}, u32[]{:S(2)}) collective-permute-start(bf16[4,32,256]{2,1,0:T(8,128)(2,1)S(1)} %get-tuple-element.13), channel_id=1, source_target_pairs={{0,32},{32,64},{64,96},{96,0},{1,33},{33,65},{65,97},{97,1},{2,34}... | collective-permute-start | bytes 196616 | tf_op jit(solution)/shard_map/ppermute | solution.py:430
  32.8 5.8 %collective-permute-start.4 = (bf16[4,32,256]{2,1,0:T(8,128)(2,1)S(1)}, bf16[4,32,256]{2,1,0:T(8,128)(2,1)S(1)}, u32[]{:S(2)}, u32[]{:S(2)}) collective-permute-start(bf16[4,32,256]{2,1,0:T(8,128)(2,1)S(1)} %get-tuple-element.14), channel_id=1, source_target_pairs={{0,64},{32,96},{64,0},{96,32},{1,65},{33,97},{65,1},{97,33},{2,66}... | collective-permute-start | bytes 196616 | tf_op jit(solution)/shard_map/ppermute | solution.py:430
  34.6 4.3 %collective-permute-start.5 = (bf16[4,32,256]{2,1,0:T(8,128)(2,1)S(1)}, bf16[4,32,256]{2,1,0:T(8,128)(2,1)S(1)}, u32[]{:S(2)}, u32[]{:S(2)}) collective-permute-start(bf16[4,32,256]{2,1,0:T(8,128)(2,1)S(1)} %get-tuple-element.15), channel_id=1, source_target_pairs={{0,96},{32,0},{64,32},{96,64},{1,97},{33,1},{65,33},{97,65},{2,98}... | collective-permute-start | bytes 196616 | tf_op jit(solution)/shard_map/ppermute | solution.py:430
  40.8 15.5 %all-to-all-start.1 = ((bf16[32,32,256]{2,1,0:T(8,128)(2,1)}), bf16[32,32,256]{2,1,0:T(8,128)(2,1)S(1)}, u32[]{:S(2)}, u32[]{:S(2)}) async-start(bf16[32,32,256]{2,1,0:T(8,128)(2,1)} %tile_terms.1), calls=%async_computation.1 | async-start | bytes 1048576 | tf_op jit(solution)/shard_map/all_to_all | solution.py:458
  56.4 4.1 %collective-permute-start.8 = (f32[32,256]{1,0:T(8,128)S(1)}, f32[32,256]{1,0:T(8,128)S(1)}, u32[]{:S(2)}, u32[]{:S(2)}) collective-permute-start(f32[32,256]{1,0:T(8,128)S(1)} %sum_band.1.refs_0_), channel_id=1, source_target_pairs={{0,96},{32,0},{64,32},{96,64},{1,97},{33,1},{65,33},{97,65},{2,98}... | collective-permute-start | bytes 98312 | tf_op jit(solution)/shard_map/ppermute | solution.py:430
  58.8 5.4 %collective-permute-start.7 = (f32[32,256]{1,0:T(8,128)S(1)}, f32[32,256]{1,0:T(8,128)S(1)}, u32[]{:S(2)}, u32[]{:S(2)}) collective-permute-start(f32[32,256]{1,0:T(8,128)S(1)} %sum_band.1.refs_0_), channel_id=1, source_target_pairs={{0,64},{32,96},{64,0},{96,32},{1,65},{33,97},{65,1},{97,33},{2,66}... | collective-permute-start | bytes 98312 | tf_op jit(solution)/shard_map/ppermute | solution.py:430
  59.5 5.1 %collective-permute-start.6 = (f32[32,256]{1,0:T(8,128)S(1)}, f32[32,256]{1,0:T(8,128)S(1)}, u32[]{:S(2)}, u32[]{:S(2)}) collective-permute-start(f32[32,256]{1,0:T(8,128)S(1)} %sum_band.1.refs_0_), channel_id=1, source_target_pairs={{0,32},{32,64},{64,96},{96,0},{1,33},{33,65},{65,97},{97,1},{2,34}... | collective-permute-start | bytes 98312 | tf_op jit(solution)/shard_map/ppermute | solution.py:430

commit v4 on v3

--- a/solution.py
+++ b/solution.py
@@ -246,7 +246,8 @@
         me = me_ref[0]
         for k in range(n_obs):
             owner = lax.rem(me - k + n_obs, n_obs)
-            full_ref[pl.ds(pl.multiple_of(owner * band, band), band), :] = band_refs[k][...]
+            rows = pl.ds(pl.multiple_of(owner * band, band), band)
+            full_ref[rows, :] = band_refs[k][...]
         curvature = full_ref[:, 0:members]
         right = full_ref[:, members:width] - curvature
         share = 1.0 / members
@@ -430,6 +431,13 @@
     return lax.ppermute(array, axis, [(i, (i + step) % n) for i in range(n)])
 
 
+def exchanged(arrays):
+    moved = []
+    for k, array in enumerate(arrays, 1):
+        moved.append(shifted(array, "obs", k))
+    return moved
+
+
 def on_device(
     log_k, heads_pred, slot_well, tile_count, obs_values, obs_std, loc_blocks, taper, lambdas
 ):
@@ -453,12 +461,12 @@
         axis=1,
     )
     grams = block_grams(place_obs, received, wells, moments, n_obs)
-    parts = [grams[0]] + [shifted(grams[k], "obs", k) for k in range(1, n_obs)]
+    parts = [grams[0]] + exchanged(grams[1:])
     terms = tile_terms(weights, parts)
     gathered = lax.all_to_all(terms, "cell", split_axis=0, concat_axis=0, tiled=True)
     moments = field_moments(log_k, moments, 2 * chunk, chunk, 4)
     own_band = sum_band(gathered, moments)
-    bands = [own_band] + [shifted(own_band, "obs", k) for k in range(1, n_obs)]
+    bands = [own_band] + exchanged([own_band] * (n_obs - 1))
     posterior, norms = finish(place_obs, lambdas, bands, moments, log_k, 6)
     return (posterior, norms[None])
 

time: 107 us -> 107 us (level)
  no operation moved by 1% of the time
where the time goes in v4:
time: 107 us
  Pallas kernels  60 us (56%)
  starting transfers between devices  25.1 us (23%)
  waiting for transfers between devices  19.9 us (19%)
  between operations  1.58 us (1%)
    pallas_call x1, Pallas kernels, finish(): pl.pallas_call(body, out_shape=[jax.ShapeDtypeStruct((cells, members), BF...  41.9 us
    ppermute x9, starting transfers between devices, shifted(): return lax.ppermute(array, axis, [(i, (i + step) % n) for i in range(n)])  12.9 us
    pallas_call x2, Pallas kernels, field_moments(): pl.pallas_call(body, out_shape=jax.ShapeDtypeStruct((members, members), F...  11.7 us
    all_to_all x1, starting transfers between devices, on_device(): lax.all_to_all(sent, 'cell', split_axis=0, concat_axis=0, tiled=True)  8.16 us
    ppermute x9, waiting for transfers between devices, shifted(): return lax.ppermute(array, axis, [(i, (i + step) % n) for i in range(n)])  8 us
    all_to_all x1, waiting for transfers between devices, on_device(): lax.all_to_all(sent, 'cell', split_axis=0, concat_axis=0, tiled=True)  7.77 us
    all_to_all x1, waiting for transfers between devices, on_device(): lax.all_to_all(terms, 'cell', split_axis=0, concat_axis=0, tiled=True)  4.11 us
    all_to_all x1, starting transfers between devices, on_device(): lax.all_to_all(terms, 'cell', split_axis=0, concat_axis=0, tiled=True)  4.07 us
  transfers between devices with their start and end apart: 11, of which 8 were waited for; matrix products, arithmetic and copies ran while one was open for 0% of the time, Pallas kernels for 11%

profile of v4, /device:TPU:0, one launch (start us, length us, event | category | flops | bytes accessed | tf_op | source)
XLA Modules:
  0.0 106.8 jit_solution(13594663899061181425)
XLA Ops:
  1.3 2.7 %send_rows.1 = (bf16[32,72,128]{2,1,0:T(8,128)(2,1)}, f32[136,128]{1,0:T(8,128)}) custom-call(s32[1]{0:T(128)S(6)} %copy.14.count_ref, s32[1,512]{1,0:T(1,128)} %bitcast.4, bf16[512,128]{1,0:T(8,128)(2,1)} %heads_ref.1, f32[128,128]{1,0:T(8,128)} %value_ref.1, f32[1,128]{1,0:T(1,128)} %bitcast.6), custom_call_target="tpu_custom_call" | custom-call | flops 1000000000 | bytes 1000000 | tf_op jit(solution)/shard_map/send_rows/pallas_call | solution.py:73
  4.0 0.0 copy-start.1
  4.0 3.1 %collective-permute-start.2 = (f32[136,128]{1,0:T(8,128)}, f32[136,128]{1,0:T(8,128)S(1)}, u32[]{:S(2)}, u32[]{:S(2)}) collective-permute-start(f32[136,128]{1,0:T(8,128)} %get-tuple-element.11.refs_0_), channel_id=1, source_target_pairs={{0,96},{32,0},{64,32},{96,64},{1,97},{33,1},{65,33},{97,65},{2,98}... | collective-permute-start | bytes 208904 | tf_op jit(solution)/shard_map/ppermute | solution.py:431
  7.1 0.6 collective-permute-start.1
  7.7 1.0 collective-permute-start
  8.7 8.2 %all-to-all-start = ((bf16[32,72,128]{2,1,0:T(8,128)(2,1)}), bf16[32,72,128]{2,1,0:T(8,128)(2,1)S(1)}, u32[]{:S(2)}, u32[]{:S(2)}) async-start(bf16[32,72,128]{2,1,0:T(8,128)(2,1)} %get-tuple-element.10), calls=%async_computation | async-start | bytes 1179648 | tf_op jit(solution)/shard_map/all_to_all | solution.py:451
  16.9 0.0 copy-start.2
  16.9 0.0 copy-start.3
  16.9 4.5 %field_moments.2.after_ref.total_ref = f32[128,128]{1,0:T(8,128)S(1)} custom-call(bf16[49152,128]{1,0:T(8,128)(2,1)} %refs_5_.1, f32[128,128]{1,0:T(8,128)S(1)} %broadcast_in_dim.4.total_ref), custom_call_target="tpu_custom_call" | custom-call | flops 6000000000 | bytes 4194304 | tf_op jit(solution)/shard_map/field_moments/pallas_call | solution.py:394
  21.4 0.0 collective-permute-done.2.refs_3_
  21.4 0.0 collective-permute-done.1.refs_2_
  21.4 0.0 collective-permute-done.refs_1_
  21.4 7.8 %all-to-all-done.recv_ref = bf16[32,72,128]{2,1,0:T(8,128)(2,1)S(1)} async-done(((bf16[32,72,128]{2,1,0:T(8,128)(2,1)}), bf16[32,72,128]{2,1,0:T(8,128)(2,1)S(1)}, u32[]{:S(2)}, u32[]{:S(2)}) %all-to-all-start) | async-done | bytes 589856 | tf_op jit(solution)/shard_map/all_to_all | solution.py:451
  29.2 0.0 copy-done.1
  29.2 1.6 %block_grams.1 = (bf16[4,32,256]{2,1,0:T(8,128)(2,1)S(1)}, bf16[4,32,256]{2,1,0:T(8,128)(2,1)S(1)}, bf16[4,32,256]{2,1,0:T(8,128)(2,1)S(1)}, bf16[4,32,256]{2,1,0:T(8,128)(2,1)S(1)}) custom-call(s32[1]{0:T(128)} %bitcast.me_ref, bf16[32,72,128]{2,1,0:T(8,128)(2,1)S(1)} %all-to-all-done.recv_ref, f32[128,128]{1,0:T(8,128)S(1)} %field_moments.2.after_ref.total_ref, ...), custom_call_target="tpu_custom_call" | custom-call | flops 1000000000 | bytes 1000000 | tf_op jit(solution)/shard_map/block_grams/pallas_call | solution.py:125
  30.8 0.0 copy-start
  30.9 2.0 %collective-permute-start.3 = (bf16[4,32,256]{2,1,0:T(8,128)(2,1)S(1)}, bf16[4,32,256]{2,1,0:T(8,128)(2,1)S(1)}, u32[]{:S(2)}, u32[]{:S(2)}) collective-permute-start(bf16[4,32,256]{2,1,0:T(8,128)(2,1)S(1)} %get-tuple-element.13), channel_id=1, source_target_pairs={{0,32},{32,64},{64,96},{96,0},{1,33},{33,65},{65,97},{97,1},{2,34}... | collective-permute-start | bytes 196616 | tf_op jit(solution)/shard_map/ppermute | solution.py:431
  32.8 1.8 %collective-permute-start.4 = (bf16[4,32,256]{2,1,0:T(8,128)(2,1)S(1)}, bf16[4,32,256]{2,1,0:T(8,128)(2,1)S(1)}, u32[]{:S(2)}, u32[]{:S(2)}) collective-permute-start(bf16[4,32,256]{2,1,0:T(8,128)(2,1)S(1)} %get-tuple-element.14), channel_id=1, source_target_pairs={{0,64},{32,96},{64,0},{96,32},{1,65},{33,97},{65,1},{97,33},{2,66}... | collective-permute-start | bytes 196616 | tf_op jit(solution)/shard_map/ppermute | solution.py:431
  34.6 0.9 collective-permute-start.5
  35.6 0.0 copy-done.2
  35.6 0.0 copy-done.3
  35.6 0.1 select_reduce_fusion
  35.7 0.1 copy.13.weight_ref
  35.8 0.6 collective-permute-done.3.refs_1_
  36.4 2.2 %collective-permute-done.4.refs_2_ = bf16[4,32,256]{2,1,0:T(8,128)(2,1)S(1)} collective-permute-done((bf16[4,32,256]{2,1,0:T(8,128)(2,1)S(1)}, bf16[4,32,256]{2,1,0:T(8,128)(2,1)S(1)}, u32[]{:S(2)}, u32[]{:S(2)}) %collective-permute-start.4) | collective-permute-done | bytes 65568 | tf_op jit(solution)/shard_map/ppermute | solution.py:431
  38.6 0.3 collective-permute-done.5.refs_3_
  38.9 1.9 %tile_terms.1 = bf16[32,32,256]{2,1,0:T(8,128)(2,1)} custom-call(f32[32,4]{1,0:T(8,128)S(1)} %copy.13.weight_ref, bf16[4,32,256]{2,1,0:T(8,128)(2,1)S(1)} %get-tuple-element.12.refs_0_, bf16[4,32,256]{2,1,0:T(8,128)(2,1)S(1)} %collective-permute-done.3.refs_1_, bf16[4,32,256]{2,1,0:T(8,128)(2,1)S(1)} %collective-permute-done.4.refs_2_, ...), custom_call_target="tpu_custom_call" | custom-call | flops 100000000 | bytes 1000000 | tf_op jit(solution)/shard_map/tile_terms/pallas_call | solution.py:155
  40.8 4.1 %all-to-all-start.1 = ((bf16[32,32,256]{2,1,0:T(8,128)(2,1)}), bf16[32,32,256]{2,1,0:T(8,128)(2,1)S(1)}, u32[]{:S(2)}, u32[]{:S(2)}) async-start(bf16[32,32,256]{2,1,0:T(8,128)(2,1)} %tile_terms.1), calls=%async_computation.1 | async-start | bytes 1048576 | tf_op jit(solution)/shard_map/all_to_all | solution.py:466
  44.9 7.3 %field_moments.3.after_ref.refs_4_ = f32[128,128]{1,0:T(8,128)S(1)} custom-call(bf16[49152,128]{1,0:T(8,128)(2,1)} %refs_5_.1, f32[128,128]{1,0:T(8,128)S(1)} %field_moments.2.after_ref.total_ref), custom_call_target="tpu_custom_call" | custom-call | flops 6000000000 | bytes 8388608 | tf_op jit(solution)/shard_map/field_moments/pallas_call | solution.py:394
  52.2 4.1 %all-to-all-done.1.gathered_ref = bf16[32,32,256]{2,1,0:T(8,128)(2,1)S(1)} async-done(((bf16[32,32,256]{2,1,0:T(8,128)(2,1)}), bf16[32,32,256]{2,1,0:T(8,128)(2,1)S(1)}, u32[]{:S(2)}, u32[]{:S(2)}) %all-to-all-start.1) | async-done | bytes 524320 | tf_op jit(solution)/shard_map/all_to_all | solution.py:466
  56.3 0.1 sum_band.1.refs_0_
  56.4 2.5 %collective-permute-start.8 = (f32[32,256]{1,0:T(8,128)S(1)}, f32[32,256]{1,0:T(8,128)S(1)}, u32[]{:S(2)}, u32[]{:S(2)}) collective-permute-start(f32[32,256]{1,0:T(8,128)S(1)} %sum_band.1.refs_0_), channel_id=1, source_target_pairs={{0,96},{32,0},{64,32},{96,64},{1,97},{33,1},{65,33},{97,65},{2,98}... | collective-permute-start | bytes 98312 | tf_op jit(solution)/shard_map/ppermute | solution.py:431
  58.8 0.7 collective-permute-start.7
  59.5 0.3 collective-permute-start.6
  59.8 0.6 collective-permute-done.8.refs_3_
  60.4 3.8 %collective-permute-done.7.refs_2_ = f32[32,256]{1,0:T(8,128)S(1)} collective-permute-done((f32[32,256]{1,0:T(8,128)S(1)}, f32[32,256]{1,0:T(8,128)S(1)}, u32[]{:S(2)}, u32[]{:S(2)}) %collective-permute-start.7) | collective-permute-done | bytes 32800 | tf_op jit(solution)/shard_map/ppermute | solution.py:431
  64.3 0.4 collective-permute-done.6.refs_1_
  64.6 0.0 copy-done
  64.6 41.9 %finish.1 = (bf16[49152,128]{1,0:T(8,128)(2,1)}, f32[4,128]{1,0:T(4,128)}) custom-call(s32[1]{0:T(128)} %bitcast.me_ref, f32[4]{0:T(128)S(1)} %copy-done, f32[32,256]{1,0:T(8,128)S(1)} %sum_band.1.refs_0_, f32[32,256]{1,0:T(8,128)S(1)} %collective-permute-done.6.refs_1_, f32[32,256]{1,0:T(8,128)S(1)} %collective-permute-done.7.refs_2_, ...), custom_call_target="tpu_custom_call" | custom-call | flops 2000000000 | bytes 25165824 | tf_op jit(solution)/shard_map/finish/pallas_call | solution.py:351
  (2 shorter events, 0.0 us)
Async XLA Ops:
  4.0 25.2 %copy-start.1 = (f32[136,128]{1,0:T(8,128)S(1)}, f32[136,128]{1,0:T(8,128)}, u32[]{:S(2)}) copy-start(f32[136,128]{1,0:T(8,128)} %get-tuple-element.11.refs_0_) | copy-start | bytes 208900
  4.0 17.4 %collective-permute-start.2 = (f32[136,128]{1,0:T(8,128)}, f32[136,128]{1,0:T(8,128)S(1)}, u32[]{:S(2)}, u32[]{:S(2)}) collective-permute-start(f32[136,128]{1,0:T(8,128)} %get-tuple-element.11.refs_0_), channel_id=1, source_target_pairs={{0,96},{32,0},{64,32},{96,64},{1,97},{33,1},{65,33},{97,65},{2,98}... | collective-permute-start | bytes 208904 | tf_op jit(solution)/shard_map/ppermute | solution.py:431
  7.1 14.3 %collective-permute-start.1 = (f32[136,128]{1,0:T(8,128)}, f32[136,128]{1,0:T(8,128)S(1)}, u32[]{:S(2)}, u32[]{:S(2)}) collective-permute-start(f32[136,128]{1,0:T(8,128)} %get-tuple-element.11.refs_0_), channel_id=1, source_target_pairs={{0,64},{32,96},{64,0},{96,32},{1,65},{33,97},{65,1},{97,33},{2,66}... | collective-permute-start | bytes 208904 | tf_op jit(solution)/shard_map/ppermute | solution.py:431
  7.7 13.7 %collective-permute-start = (f32[136,128]{1,0:T(8,128)}, f32[136,128]{1,0:T(8,128)S(1)}, u32[]{:S(2)}, u32[]{:S(2)}) collective-permute-start(f32[136,128]{1,0:T(8,128)} %get-tuple-element.11.refs_0_), channel_id=1, source_target_pairs={{0,32},{32,64},{64,96},{96,0},{1,33},{33,65},{65,97},{97,1},{2,34}... | collective-permute-start | bytes 208904 | tf_op jit(solution)/shard_map/ppermute | solution.py:431
  8.7 20.5 %all-to-all-start = ((bf16[32,72,128]{2,1,0:T(8,128)(2,1)}), bf16[32,72,128]{2,1,0:T(8,128)(2,1)S(1)}, u32[]{:S(2)}, u32[]{:S(2)}) async-start(bf16[32,72,128]{2,1,0:T(8,128)(2,1)} %get-tuple-element.10), calls=%async_computation | async-start | bytes 1179648 | tf_op jit(solution)/shard_map/all_to_all | solution.py:451
  16.9 18.7 %copy-start.2 = (f32[32,8]{0,1:T(8,128)S(1)}, f32[32,8]{0,1:T(8,128)}, u32[]{:S(2)}) copy-start(f32[32,8]{0,1:T(8,128)} %param.16) | copy-start | bytes 3076
  16.9 18.7 %copy-start.3 = (s32[32,8]{0,1:T(8,128)S(1)}, s32[32,8]{0,1:T(8,128)}, u32[]{:S(2)}) copy-start(s32[32,8]{0,1:T(8,128)} %param.15) | copy-start | bytes 3076
  30.8 33.8 %copy-start = (f32[4]{0:T(128)S(1)}, f32[4]{0:T(128)}, u32[]{:S(2)}) copy-start(f32[4]{0:T(128)} %lam_ref.1) | copy-start | bytes 52
  30.9 5.5 %collective-permute-start.3 = (bf16[4,32,256]{2,1,0:T(8,128)(2,1)S(1)}, bf16[4,32,256]{2,1,0:T(8,128)(2,1)S(1)}, u32[]{:S(2)}, u32[]{:S(2)}) collective-permute-start(bf16[4,32,256]{2,1,0:T(8,128)(2,1)S(1)} %get-tuple-element.13), channel_id=1, source_target_pairs={{0,32},{32,64},{64,96},{96,0},{1,33},{33,65},{65,97},{97,1},{2,34}... | collective-permute-start | bytes 196616 | tf_op jit(solution)/shard_map/ppermute | solution.py:431
  32.8 5.8 %collective-permute-start.4 = (bf16[4,32,256]{2,1,0:T(8,128)(2,1)S(1)}, bf16[4,32,256]{2,1,0:T(8,128)(2,1)S(1)}, u32[]{:S(2)}, u32[]{:S(2)}) collective-permute-start(bf16[4,32,256]{2,1,0:T(8,128)(2,1)S(1)} %get-tuple-element.14), channel_id=1, source_target_pairs={{0,64},{32,96},{64,0},{96,32},{1,65},{33,97},{65,1},{97,33},{2,66}... | collective-permute-start | bytes 196616 | tf_op jit(solution)/shard_map/ppermute | solution.py:431
  34.6 4.3 %collective-permute-start.5 = (bf16[4,32,256]{2,1,0:T(8,128)(2,1)S(1)}, bf16[4,32,256]{2,1,0:T(8,128)(2,1)S(1)}, u32[]{:S(2)}, u32[]{:S(2)}) collective-permute-start(bf16[4,32,256]{2,1,0:T(8,128)(2,1)S(1)} %get-tuple-element.15), channel_id=1, source_target_pairs={{0,96},{32,0},{64,32},{96,64},{1,97},{33,1},{65,33},{97,65},{2,98}... | collective-permute-start | bytes 196616 | tf_op jit(solution)/shard_map/ppermute | solution.py:431
  40.8 15.5 %all-to-all-start.1 = ((bf16[32,32,256]{2,1,0:T(8,128)(2,1)}), bf16[32,32,256]{2,1,0:T(8,128)(2,1)S(1)}, u32[]{:S(2)}, u32[]{:S(2)}) async-start(bf16[32,32,256]{2,1,0:T(8,128)(2,1)} %tile_terms.1), calls=%async_computation.1 | async-start | bytes 1048576 | tf_op jit(solution)/shard_map/all_to_all | solution.py:466
  56.4 4.1 %collective-permute-start.8 = (f32[32,256]{1,0:T(8,128)S(1)}, f32[32,256]{1,0:T(8,128)S(1)}, u32[]{:S(2)}, u32[]{:S(2)}) collective-permute-start(f32[32,256]{1,0:T(8,128)S(1)} %sum_band.1.refs_0_), channel_id=1, source_target_pairs={{0,96},{32,0},{64,32},{96,64},{1,97},{33,1},{65,33},{97,65},{2,98}... | collective-permute-start | bytes 98312 | tf_op jit(solution)/shard_map/ppermute | solution.py:431
  58.8 5.4 %collective-permute-start.7 = (f32[32,256]{1,0:T(8,128)S(1)}, f32[32,256]{1,0:T(8,128)S(1)}, u32[]{:S(2)}, u32[]{:S(2)}) collective-permute-start(f32[32,256]{1,0:T(8,128)S(1)} %sum_band.1.refs_0_), channel_id=1, source_target_pairs={{0,64},{32,96},{64,0},{96,32},{1,65},{33,97},{65,1},{97,33},{2,66}... | collective-permute-start | bytes 98312 | tf_op jit(solution)/shard_map/ppermute | solution.py:431
  59.5 5.1 %collective-permute-start.6 = (f32[32,256]{1,0:T(8,128)S(1)}, f32[32,256]{1,0:T(8,128)S(1)}, u32[]{:S(2)}, u32[]{:S(2)}) collective-permute-start(f32[32,256]{1,0:T(8,128)S(1)} %sum_band.1.refs_0_), channel_id=1, source_target_pairs={{0,32},{32,64},{64,96},{96,0},{1,33},{33,65},{65,97},{97,1},{2,34}... | collective-permute-start | bytes 98312 | tf_op jit(solution)/shard_map/ppermute | solution.py:431

commit v5 on v4

--- a/solution.py
+++ b/solution.py
@@ -10,6 +10,7 @@
 EXTRA = 8
 SPREAD = 16
 TILE = 512
+PARTS = 2
 F32 = jnp.float32
 BF16 = jnp.bfloat16
 HIGHEST = lax.Precision.HIGHEST
@@ -41,12 +42,22 @@
     return pl.CostEstimate(flops=int(flops), bytes_accessed=int(size), transcendentals=0)
 
 
+def in_parts(source, target, sem):
+    length = source.shape[0] // PARTS
+    spans = [pl.ds(i * length, length) for i in range(PARTS)]
+    return [
+        pltpu.make_async_copy(source.at[span], target.at[span], sem.at[i])
+        for i, span in enumerate(spans)
+    ]
+
+
 def send_rows(slot_well, tile_count, heads, obs_values, obs_std, n_obs, n_cell):
     slots, members = heads.shape
     wells_dev = obs_values.shape[0]
     rows = n_obs * CAP
 
-    def body(count_ref, well_ref, heads_ref, value_ref, std_ref, out_ref, join_ref):
+    def body(count_ref, well_ref, heads_ref, value_ref, std_ref, out_ref, join_ref, hold_ref, sem):
+        copies = in_parts(hold_ref, out_ref, sem)
         well = well_ref[...]
         valid = iota((1, slots), 1) < count_ref[0]
         block = jnp.where(valid, well // wells_dev, -1)
@@ -63,12 +74,16 @@
         values = heads_ref[...]
         for c in range(n_cell):
             pick = one_hot(iota((rows, slots), 0) + c * rows == target)
-            out_ref[c, 0:rows, :] = dot(pick, values).astype(BF16)
-            out_ref[c, rows : rows + EXTRA, :] = jnp.broadcast_to(
+            hold_ref[c, 0:rows, :] = dot(pick, values).astype(BF16)
+            hold_ref[c, rows : rows + EXTRA, :] = jnp.broadcast_to(
                 places[c : c + 1, :], (EXTRA, members)
             ).astype(BF16)
+            if (c + 1) % (n_cell // PARTS) == 0:
+                copies[c // (n_cell // PARTS)].start()
         join_ref[0:wells_dev, :] = value_ref[...]
         join_ref[wells_dev:, :] = jnp.broadcast_to(std_ref[...], (EXTRA, wells_dev))
+        for copy in copies:
+            copy.wait()
 
     return pl.pallas_call(
         body,
@@ -77,7 +92,11 @@
             jax.ShapeDtypeStruct((wells_dev + EXTRA, members), F32),
         ],
         in_specs=[SMEM] + [VMEM] * 4,
-        out_specs=[VMEM, VMEM],
+        out_specs=[ANY, VMEM],
+        scratch_shapes=[
+            pltpu.VMEM((n_cell, rows + EXTRA, members), BF16),
+            pltpu.SemaphoreType.DMA((PARTS,)),
+        ],
         compiler_params=params(60),
         cost_estimate=cost(1e9, 1e6),
         name="send_rows",
@@ -139,24 +158,33 @@
     _, band, width = parts[0].shape
 
     def body(weight_ref, *refs):
-        out_ref = refs[-1]
+        out_ref, hold_ref, sem = refs[-3:]
+        copies = in_parts(hold_ref, out_ref, sem)
         totals = []
         for o in range(n_obs):
             total = refs[0][o].astype(F32)
-            for ref in refs[1:-1]:
+            for ref in refs[1:-3]:
                 total = total + ref[o].astype(F32)
             totals.append(total)
         for t in range(n_tiles):
             term = weight_ref[t, 0] * totals[0]
             for o in range(1, n_obs):
                 term = term + weight_ref[t, o] * totals[o]
-            out_ref[t] = term.astype(BF16)
+            hold_ref[t] = term.astype(BF16)
+            if (t + 1) % (n_tiles // PARTS) == 0:
+                copies[t // (n_tiles // PARTS)].start()
+        for copy in copies:
+            copy.wait()
 
     return pl.pallas_call(
         body,
         out_shape=jax.ShapeDtypeStruct((n_tiles, band, width), BF16),
         in_specs=[SMEM] + [VMEM] * len(parts),
-        out_specs=VMEM,
+        out_specs=ANY,
+        scratch_shapes=[
+            pltpu.VMEM((n_tiles, band, width), BF16),
+            pltpu.SemaphoreType.DMA((PARTS,)),
+        ],
         compiler_params=params(16),
         cost_estimate=cost(1e8, 1e6),
         name="tile_terms",

time: 107 us -> 108 us (level)
  no operation moved by 1% of the time
where the time goes in v5:
time: 108 us; the launch traced here: 107 us
  Pallas kernels  60.5 us (56%)
  starting transfers between devices  25.2 us (23%)
  waiting for transfers between devices  19.9 us (18%)
  between operations  1.6 us (1%)
    pallas_call x1, Pallas kernels, finish(): pl.pallas_call(body, out_shape=[jax.ShapeDtypeStruct((cells, members), BF...  41.9 us
    ppermute x9, starting transfers between devices, shifted(): return lax.ppermute(array, axis, [(i, (i + step) % n) for i in range(n)])  12.9 us
    pallas_call x2, Pallas kernels, field_moments(): pl.pallas_call(body, out_shape=jax.ShapeDtypeStruct((members, members), F...  11.7 us
    all_to_all x1, starting transfers between devices, on_device(): lax.all_to_all(sent, 'cell', split_axis=0, concat_axis=0, tiled=True)  8.16 us
    ppermute x9, waiting for transfers between devices, shifted(): return lax.ppermute(array, axis, [(i, (i + step) % n) for i in range(n)])  8.01 us
    all_to_all x1, waiting for transfers between devices, on_device(): lax.all_to_all(sent, 'cell', split_axis=0, concat_axis=0, tiled=True)  7.77 us
    all_to_all x1, waiting for transfers between devices, on_device(): lax.all_to_all(terms, 'cell', split_axis=0, concat_axis=0, tiled=True)  4.11 us
    all_to_all x1, starting transfers between devices, on_device(): lax.all_to_all(terms, 'cell', split_axis=0, concat_axis=0, tiled=True)  4.08 us
  transfers between devices with their start and end apart: 11, of which 8 were waited for; matrix products, arithmetic and copies ran while one was open for 0% of the time, Pallas kernels for 11%

profile of v5, /device:TPU:0, one launch (start us, length us, event | category | flops | bytes accessed | tf_op | source)
XLA Modules:
  0.0 107.3 jit_solution(17892854183112976650)
XLA Ops:
  1.3 3.2 %send_rows.1 = (bf16[32,72,128]{2,1,0:T(8,128)(2,1)}, f32[136,128]{1,0:T(8,128)}) custom-call(s32[1]{0:T(128)S(6)} %copy.14.count_ref, s32[1,512]{1,0:T(1,128)} %bitcast.4, bf16[512,128]{1,0:T(8,128)(2,1)} %heads_ref.1, f32[128,128]{1,0:T(8,128)} %value_ref.1, f32[1,128]{1,0:T(1,128)} %bitcast.6), custom_call_target="tpu_custom_call" | custom-call | flops 1000000000 | bytes 1000000 | tf_op jit(solution)/shard_map/send_rows/pallas_call | solution.py:88
  4.5 0.0 copy-start.1
  4.5 3.2 %collective-permute-start.2 = (f32[136,128]{1,0:T(8,128)}, f32[136,128]{1,0:T(8,128)S(1)}, u32[]{:S(2)}, u32[]{:S(2)}) collective-permute-start(f32[136,128]{1,0:T(8,128)} %get-tuple-element.11.refs_0_), channel_id=1, source_target_pairs={{0,96},{32,0},{64,32},{96,64},{1,97},{33,1},{65,33},{97,65},{2,98}... | collective-permute-start | bytes 208904 | tf_op jit(solution)/shard_map/ppermute | solution.py:459
  7.7 0.6 collective-permute-start.1
  8.4 1.0 collective-permute-start
  9.3 8.2 %all-to-all-start = ((bf16[32,72,128]{2,1,0:T(8,128)(2,1)}), bf16[32,72,128]{2,1,0:T(8,128)(2,1)S(1)}, u32[]{:S(2)}, u32[]{:S(2)}) async-start(bf16[32,72,128]{2,1,0:T(8,128)(2,1)} %get-tuple-element.10), calls=%async_computation | async-start | bytes 1179648 | tf_op jit(solution)/shard_map/all_to_all | solution.py:479
  17.5 0.0 copy-start.2
  17.5 0.0 copy-start.3
  17.5 4.5 %field_moments.2.after_ref.total_ref = f32[128,128]{1,0:T(8,128)S(1)} custom-call(bf16[49152,128]{1,0:T(8,128)(2,1)} %refs_5_.1, f32[128,128]{1,0:T(8,128)S(1)} %broadcast_in_dim.4.total_ref), custom_call_target="tpu_custom_call" | custom-call | flops 6000000000 | bytes 4194304 | tf_op jit(solution)/shard_map/field_moments/pallas_call | solution.py:422
  22.0 0.0 collective-permute-done.2.refs_3_
  22.0 0.0 collective-permute-done.1.refs_2_
  22.0 0.0 collective-permute-done.refs_1_
  22.1 7.8 %all-to-all-done.recv_ref = bf16[32,72,128]{2,1,0:T(8,128)(2,1)S(1)} async-done(((bf16[32,72,128]{2,1,0:T(8,128)(2,1)}), bf16[32,72,128]{2,1,0:T(8,128)(2,1)S(1)}, u32[]{:S(2)}, u32[]{:S(2)}) %all-to-all-start) | async-done | bytes 589856 | tf_op jit(solution)/shard_map/all_to_all | solution.py:479
  29.8 0.0 copy-done.1
  29.8 1.6 %block_grams.1 = (bf16[4,32,256]{2,1,0:T(8,128)(2,1)S(1)}, bf16[4,32,256]{2,1,0:T(8,128)(2,1)S(1)}, bf16[4,32,256]{2,1,0:T(8,128)(2,1)S(1)}, bf16[4,32,256]{2,1,0:T(8,128)(2,1)S(1)}) custom-call(s32[1]{0:T(128)} %bitcast.me_ref, bf16[32,72,128]{2,1,0:T(8,128)(2,1)S(1)} %all-to-all-done.recv_ref, f32[128,128]{1,0:T(8,128)S(1)} %field_moments.2.after_ref.total_ref, ...), custom_call_target="tpu_custom_call" | custom-call | flops 1000000000 | bytes 1000000 | tf_op jit(solution)/shard_map/block_grams/pallas_call | solution.py:144
  31.5 0.0 copy-start
  31.5 2.0 %collective-permute-start.3 = (bf16[4,32,256]{2,1,0:T(8,128)(2,1)S(1)}, bf16[4,32,256]{2,1,0:T(8,128)(2,1)S(1)}, u32[]{:S(2)}, u32[]{:S(2)}) collective-permute-start(bf16[4,32,256]{2,1,0:T(8,128)(2,1)S(1)} %get-tuple-element.13), channel_id=1, source_target_pairs={{0,32},{32,64},{64,96},{96,0},{1,33},{33,65},{65,97},{97,1},{2,34}... | collective-permute-start | bytes 196616 | tf_op jit(solution)/shard_map/ppermute | solution.py:459
  33.4 1.8 %collective-permute-start.4 = (bf16[4,32,256]{2,1,0:T(8,128)(2,1)S(1)}, bf16[4,32,256]{2,1,0:T(8,128)(2,1)S(1)}, u32[]{:S(2)}, u32[]{:S(2)}) collective-permute-start(bf16[4,32,256]{2,1,0:T(8,128)(2,1)S(1)} %get-tuple-element.14), channel_id=1, source_target_pairs={{0,64},{32,96},{64,0},{96,32},{1,65},{33,97},{65,1},{97,33},{2,66}... | collective-permute-start | bytes 196616 | tf_op jit(solution)/shard_map/ppermute | solution.py:459
  35.3 0.9 collective-permute-start.5
  36.2 0.0 copy-done.2
  36.2 0.0 copy-done.3
  36.2 0.1 select_reduce_fusion
  36.3 0.1 copy.13.weight_ref
  36.4 0.6 collective-permute-done.3.refs_1_
  37.0 2.2 %collective-permute-done.4.refs_2_ = bf16[4,32,256]{2,1,0:T(8,128)(2,1)S(1)} collective-permute-done((bf16[4,32,256]{2,1,0:T(8,128)(2,1)S(1)}, bf16[4,32,256]{2,1,0:T(8,128)(2,1)S(1)}, u32[]{:S(2)}, u32[]{:S(2)}) %collective-permute-start.4) | collective-permute-done | bytes 65568 | tf_op jit(solution)/shard_map/ppermute | solution.py:459
  39.2 0.3 collective-permute-done.5.refs_3_
  39.6 1.8 %tile_terms.1 = bf16[32,32,256]{2,1,0:T(8,128)(2,1)} custom-call(f32[32,4]{1,0:T(8,128)S(1)} %copy.13.weight_ref, bf16[4,32,256]{2,1,0:T(8,128)(2,1)S(1)} %get-tuple-element.12.refs_0_, bf16[4,32,256]{2,1,0:T(8,128)(2,1)S(1)} %collective-permute-done.3.refs_1_, bf16[4,32,256]{2,1,0:T(8,128)(2,1)S(1)} %collective-permute-done.4.refs_2_, ...), custom_call_target="tpu_custom_call" | custom-call | flops 100000000 | bytes 1000000 | tf_op jit(solution)/shard_map/tile_terms/pallas_call | solution.py:179
  41.4 4.1 %all-to-all-start.1 = ((bf16[32,32,256]{2,1,0:T(8,128)(2,1)}), bf16[32,32,256]{2,1,0:T(8,128)(2,1)S(1)}, u32[]{:S(2)}, u32[]{:S(2)}) async-start(bf16[32,32,256]{2,1,0:T(8,128)(2,1)} %tile_terms.1), calls=%async_computation.1 | async-start | bytes 1048576 | tf_op jit(solution)/shard_map/all_to_all | solution.py:494
  45.5 7.3 %field_moments.3.after_ref.refs_4_ = f32[128,128]{1,0:T(8,128)S(1)} custom-call(bf16[49152,128]{1,0:T(8,128)(2,1)} %refs_5_.1, f32[128,128]{1,0:T(8,128)S(1)} %field_moments.2.after_ref.total_ref), custom_call_target="tpu_custom_call" | custom-call | flops 6000000000 | bytes 8388608 | tf_op jit(solution)/shard_map/field_moments/pallas_call | solution.py:422
  52.8 4.1 %all-to-all-done.1.gathered_ref = bf16[32,32,256]{2,1,0:T(8,128)(2,1)S(1)} async-done(((bf16[32,32,256]{2,1,0:T(8,128)(2,1)}), bf16[32,32,256]{2,1,0:T(8,128)(2,1)S(1)}, u32[]{:S(2)}, u32[]{:S(2)}) %all-to-all-start.1) | async-done | bytes 524320 | tf_op jit(solution)/shard_map/all_to_all | solution.py:494
  56.9 0.1 sum_band.1.refs_0_
  57.0 2.4 %collective-permute-start.8 = (f32[32,256]{1,0:T(8,128)S(1)}, f32[32,256]{1,0:T(8,128)S(1)}, u32[]{:S(2)}, u32[]{:S(2)}) collective-permute-start(f32[32,256]{1,0:T(8,128)S(1)} %sum_band.1.refs_0_), channel_id=1, source_target_pairs={{0,96},{32,0},{64,32},{96,64},{1,97},{33,1},{65,33},{97,65},{2,98}... | collective-permute-start | bytes 98312 | tf_op jit(solution)/shard_map/ppermute | solution.py:459
  59.4 0.7 collective-permute-start.7
  60.1 0.3 collective-permute-start.6
  60.4 0.6 collective-permute-done.8.refs_3_
  61.0 3.8 %collective-permute-done.7.refs_2_ = f32[32,256]{1,0:T(8,128)S(1)} collective-permute-done((f32[32,256]{1,0:T(8,128)S(1)}, f32[32,256]{1,0:T(8,128)S(1)}, u32[]{:S(2)}, u32[]{:S(2)}) %collective-permute-start.7) | collective-permute-done | bytes 32800 | tf_op jit(solution)/shard_map/ppermute | solution.py:459
  64.8 0.4 collective-permute-done.6.refs_1_
  65.2 0.0 copy-done
  65.2 41.9 %finish.1 = (bf16[49152,128]{1,0:T(8,128)(2,1)}, f32[4,128]{1,0:T(4,128)}) custom-call(s32[1]{0:T(128)} %bitcast.me_ref, f32[4]{0:T(128)S(1)} %copy-done, f32[32,256]{1,0:T(8,128)S(1)} %sum_band.1.refs_0_, f32[32,256]{1,0:T(8,128)S(1)} %collective-permute-done.6.refs_1_, f32[32,256]{1,0:T(8,128)S(1)} %collective-permute-done.7.refs_2_, ...), custom_call_target="tpu_custom_call" | custom-call | flops 2000000000 | bytes 25165824 | tf_op jit(solution)/shard_map/finish/pallas_call | solution.py:379
  (2 shorter events, 0.0 us)
Async XLA Ops:
  4.5 25.3 %copy-start.1 = (f32[136,128]{1,0:T(8,128)S(1)}, f32[136,128]{1,0:T(8,128)}, u32[]{:S(2)}) copy-start(f32[136,128]{1,0:T(8,128)} %get-tuple-element.11.refs_0_) | copy-start | bytes 208900
  4.5 17.5 %collective-permute-start.2 = (f32[136,128]{1,0:T(8,128)}, f32[136,128]{1,0:T(8,128)S(1)}, u32[]{:S(2)}, u32[]{:S(2)}) collective-permute-start(f32[136,128]{1,0:T(8,128)} %get-tuple-element.11.refs_0_), channel_id=1, source_target_pairs={{0,96},{32,0},{64,32},{96,64},{1,97},{33,1},{65,33},{97,65},{2,98}... | collective-permute-start | bytes 208904 | tf_op jit(solution)/shard_map/ppermute | solution.py:459
  7.7 14.3 %collective-permute-start.1 = (f32[136,128]{1,0:T(8,128)}, f32[136,128]{1,0:T(8,128)S(1)}, u32[]{:S(2)}, u32[]{:S(2)}) collective-permute-start(f32[136,128]{1,0:T(8,128)} %get-tuple-element.11.refs_0_), channel_id=1, source_target_pairs={{0,64},{32,96},{64,0},{96,32},{1,65},{33,97},{65,1},{97,33},{2,66}... | collective-permute-start | bytes 208904 | tf_op jit(solution)/shard_map/ppermute | solution.py:459
  8.4 13.7 %collective-permute-start = (f32[136,128]{1,0:T(8,128)}, f32[136,128]{1,0:T(8,128)S(1)}, u32[]{:S(2)}, u32[]{:S(2)}) collective-permute-start(f32[136,128]{1,0:T(8,128)} %get-tuple-element.11.refs_0_), channel_id=1, source_target_pairs={{0,32},{32,64},{64,96},{96,0},{1,33},{33,65},{65,97},{97,1},{2,34}... | collective-permute-start | bytes 208904 | tf_op jit(solution)/shard_map/ppermute | solution.py:459
  9.3 20.5 %all-to-all-start = ((bf16[32,72,128]{2,1,0:T(8,128)(2,1)}), bf16[32,72,128]{2,1,0:T(8,128)(2,1)S(1)}, u32[]{:S(2)}, u32[]{:S(2)}) async-start(bf16[32,72,128]{2,1,0:T(8,128)(2,1)} %get-tuple-element.10), calls=%async_computation | async-start | bytes 1179648 | tf_op jit(solution)/shard_map/all_to_all | solution.py:479
  17.5 18.7 %copy-start.2 = (f32[32,8]{0,1:T(8,128)S(1)}, f32[32,8]{0,1:T(8,128)}, u32[]{:S(2)}) copy-start(f32[32,8]{0,1:T(8,128)} %param.16) | copy-start | bytes 3076
  17.5 18.7 %copy-start.3 = (s32[32,8]{0,1:T(8,128)S(1)}, s32[32,8]{0,1:T(8,128)}, u32[]{:S(2)}) copy-start(s32[32,8]{0,1:T(8,128)} %param.15) | copy-start | bytes 3076
  31.5 33.7 %copy-start = (f32[4]{0:T(128)S(1)}, f32[4]{0:T(128)}, u32[]{:S(2)}) copy-start(f32[4]{0:T(128)} %lam_ref.1) | copy-start | bytes 52
  31.5 5.5 %collective-permute-start.3 = (bf16[4,32,256]{2,1,0:T(8,128)(2,1)S(1)}, bf16[4,32,256]{2,1,0:T(8,128)(2,1)S(1)}, u32[]{:S(2)}, u32[]{:S(2)}) collective-permute-start(bf16[4,32,256]{2,1,0:T(8,128)(2,1)S(1)} %get-tuple-element.13), channel_id=1, source_target_pairs={{0,32},{32,64},{64,96},{96,0},{1,33},{33,65},{65,97},{97,1},{2,34}... | collective-permute-start | bytes 196616 | tf_op jit(solution)/shard_map/ppermute | solution.py:459
  33.4 5.8 %collective-permute-start.4 = (bf16[4,32,256]{2,1,0:T(8,128)(2,1)S(1)}, bf16[4,32,256]{2,1,0:T(8,128)(2,1)S(1)}, u32[]{:S(2)}, u32[]{:S(2)}) collective-permute-start(bf16[4,32,256]{2,1,0:T(8,128)(2,1)S(1)} %get-tuple-element.14), channel_id=1, source_target_pairs={{0,64},{32,96},{64,0},{96,32},{1,65},{33,97},{65,1},{97,33},{2,66}... | collective-permute-start | bytes 196616 | tf_op jit(solution)/shard_map/ppermute | solution.py:459
  35.3 4.3 %collective-permute-start.5 = (bf16[4,32,256]{2,1,0:T(8,128)(2,1)S(1)}, bf16[4,32,256]{2,1,0:T(8,128)(2,1)S(1)}, u32[]{:S(2)}, u32[]{:S(2)}) collective-permute-start(bf16[4,32,256]{2,1,0:T(8,128)(2,1)S(1)} %get-tuple-element.15), channel_id=1, source_target_pairs={{0,96},{32,0},{64,32},{96,64},{1,97},{33,1},{65,33},{97,65},{2,98}... | collective-permute-start | bytes 196616 | tf_op jit(solution)/shard_map/ppermute | solution.py:459
  41.4 15.5 %all-to-all-start.1 = ((bf16[32,32,256]{2,1,0:T(8,128)(2,1)}), bf16[32,32,256]{2,1,0:T(8,128)(2,1)S(1)}, u32[]{:S(2)}, u32[]{:S(2)}) async-start(bf16[32,32,256]{2,1,0:T(8,128)(2,1)} %tile_terms.1), calls=%async_computation.1 | async-start | bytes 1048576 | tf_op jit(solution)/shard_map/all_to_all | solution.py:494
  57.0 4.0 %collective-permute-start.8 = (f32[32,256]{1,0:T(8,128)S(1)}, f32[32,256]{1,0:T(8,128)S(1)}, u32[]{:S(2)}, u32[]{:S(2)}) collective-permute-start(f32[32,256]{1,0:T(8,128)S(1)} %sum_band.1.refs_0_), channel_id=1, source_target_pairs={{0,96},{32,0},{64,32},{96,64},{1,97},{33,1},{65,33},{97,65},{2,98}... | collective-permute-start | bytes 98312 | tf_op jit(solution)/shard_map/ppermute | solution.py:459
  59.4 5.4 %collective-permute-start.7 = (f32[32,256]{1,0:T(8,128)S(1)}, f32[32,256]{1,0:T(8,128)S(1)}, u32[]{:S(2)}, u32[]{:S(2)}) collective-permute-start(f32[32,256]{1,0:T(8,128)S(1)} %sum_band.1.refs_0_), channel_id=1, source_target_pairs={{0,64},{32,96},{64,0},{96,32},{1,65},{33,97},{65,1},{97,33},{2,66}... | collective-permute-start | bytes 98312 | tf_op jit(solution)/shard_map/ppermute | solution.py:459
  60.1 5.1 %collective-permute-start.6 = (f32[32,256]{1,0:T(8,128)S(1)}, f32[32,256]{1,0:T(8,128)S(1)}, u32[]{:S(2)}, u32[]{:S(2)}) collective-permute-start(f32[32,256]{1,0:T(8,128)S(1)} %sum_band.1.refs_0_), channel_id=1, source_target_pairs={{0,32},{32,64},{64,96},{96,0},{1,33},{33,65},{65,97},{97,1},{2,34}... | collective-permute-start | bytes 98312 | tf_op jit(solution)/shard_map/ppermute | solution.py:459
